TPU v7x, 128 devices: a whole 4x4x4 slice. The times are simulated.
128 devices in a mesh: pts: 32 (over x, y, core), cam: 4 (over z).
Axes of the slice: x: 4, y: 4, z: 4, core: 2. Of those that a mesh axis runs over, the one named last changes fastest.
Arguments:
- cameras: float32 [9, 16384], P(None, ('pts', 'cam')), may hold values from -0.5 to 2
- increment: float32 [9, 16384], P(None, ('pts', 'cam')), may hold values from -0.3 to 0.3
- points: float32 [3, 2097152], P(None, 'pts'), may hold values from -6 to 2
- point_gradient: float32 [3, 2097152], P(None, 'pts'), may hold values from -1.8 to 1.8
- point_inverse: float32 [9, 2097152], P(None, 'pts'), may hold values from -0.35 to 1.6, as said below
- cam_jacobian: bfloat16 [18, 33554432], P(None, ('pts', 'cam')), may hold values from -3 to 3
- point_jacobian: bfloat16 [6, 33554432], P(None, ('pts', 'cam')), may hold values from -3 to 3
- observed: float32 [2, 33554432], P(None, ('pts', 'cam')), may hold values from -10 to 10
- tile_block: int32 [131072], P(('pts', 'cam')), may hold values from 0 to 127
- tile_points: int32 [131072], P(('pts', 'cam')), may hold values from 0 to 255
- obs_camera: int32 [33554432], P(('pts', 'cam')), may hold values from 0 to 127
- obs_point: int32 [33554432], P(('pts', 'cam')), may hold values from 0 to 255
- accept: int32 [], replicated, may hold values from 0 to 1073741823
Outputs:
- residual: float32 [2, 33554432], P(None, ('pts', 'cam'))
- trial_cost: float32 [], replicated
- accepted_points: float32 [3, 2097152], P(None, 'pts')
- accepted_cameras: float32 [9, 16384], P(None, ('pts', 'cam'))
Inputs may be any that keep to these rules, and one draw needn't show every extreme that they name: `tile_block`: the block of 128 cameras that all 256 observations of a tile look at. `tile_points`: the block of 256 points of its point group that all 256 observations of a tile look at. `obs_camera`: an observation's camera within its tile's block. `obs_point`: an observation's point within its tile's point block. `accept`: an odd word accepts the step, an even one keeps the old parameters. `point_inverse`: each 3 x 3 block is symmetric with a dominant positive diagonal.
All inputs are finite; a program needn't handle non-finite values.
Results may differ from a plain program's by a relative error of at most 0.0003.
Values sent between devices are 32-bit elements; how exact they have to be, the bound alone decides.
A program may use at most 192 MiB of HBM per device.

v0:
```python
import math

import jax
import jax.numpy as jnp
from jax import lax
from jax.sharding import Mesh
from jax.sharding import PartitionSpec as P

CB = 128
PB = 256
TILE = 256
PTS = ("pts_0", "pts_1", "pts_2")
PTS_CAM = ("pts_0", "pts_1", "pts_2", "cam")


def side_by_side(arrays, axis, dim, along):
    both = jnp.concatenate(arrays, axis=along)
    filled, at, gathered = (lax.all_gather(both, axis, axis=dim, tiled=True), 0, [])
    for a in arrays:
        gathered.append(lax.slice_in_dim(filled, at, at + a.shape[along], axis=along))
        at += a.shape[along]
    return tuple(gathered)


def in_order(pieces, dim):
    pieces = jnp.moveaxis(pieces, 0, dim)
    shape = pieces.shape
    return pieces.reshape(*shape[:dim], shape[dim] * shape[dim + 1], *shape[dim + 2 :])


def copy_for_each(array, axis):
    copies = jnp.broadcast_to(array, (lax.axis_size(axis), *array.shape))
    return lax.all_to_all(copies, axis, split_axis=0, concat_axis=0, tiled=True)


def gathered_copies(array, axis, dim):
    return in_order(copy_for_each(array, axis), dim)


def side_by_side_2(arrays, axis, dim, along):
    both = jnp.concatenate(arrays, axis=along)
    filled, at, gathered = (gathered_copies(both, axis, dim), 0, [])
    for a in arrays:
        gathered.append(lax.slice_in_dim(filled, at, at + a.shape[along], axis=along))
        at += a.shape[along]
    return tuple(gathered)


def over_pieces(array, axis):
    return lax.all_gather(array, axis).sum(0)


def one_axis_at_a_time(array, axes):
    for axis in axes:
        array = lax.psum(array, axis)
    return array


def rotate_point(angles, coords):
    angle_size = jnp.sqrt(jnp.sum(angles * angles, axis=0))
    cosine = jnp.cos(angle_size)
    sine_ratio = jnp.sinc(angle_size / math.pi)
    cosine_ratio = 0.5 * jnp.square(jnp.sinc(angle_size / (2.0 * math.pi)))
    crossed = jnp.stack(
        [
            angles[1] * coords[2] - angles[2] * coords[1],
            angles[2] * coords[0] - angles[0] * coords[2],
            angles[0] * coords[1] - angles[1] * coords[0],
        ]
    )
    inner_part = jnp.sum(angles * coords, axis=0)
    return cosine * coords + sine_ratio * crossed + cosine_ratio * inner_part * angles


def project(camera, coords):
    placed = rotate_point(camera[0:3], coords) + camera[3:6]
    depth_clip = jnp.maximum(-placed[2], 1.0)
    planar = placed[0:2] / depth_clip
    radius = jnp.sum(planar * planar, axis=0)
    factor = camera[6] * (1.0 + camera[7] * radius + camera[8] * radius * radius)
    return factor * planar


def couple(cam_rows, point_rows, cam_steps):
    cam_rows = cam_rows.astype(jnp.float32)
    point_rows = point_rows.astype(jnp.float32)
    first_row = jnp.sum(cam_rows[0:9] * cam_steps, axis=0)
    second_row = jnp.sum(cam_rows[9:18] * cam_steps, axis=0)
    return point_rows[0:3] * first_row + point_rows[3:6] * second_row


def solve_points(inverse, gradient, reduced):
    residue = gradient - reduced
    return jnp.stack(
        [
            inverse[3 * target] * residue[0]
            + inverse[3 * target + 1] * residue[1]
            + inverse[3 * target + 2] * residue[2]
            for target in range(3)
        ]
    )


def tile_onehot(local_ids, per_turn, width):
    columns = lax.iota(jnp.int32, width)
    return (local_ids.reshape(per_turn, 1, TILE) == columns.reshape(1, width, 1)).astype(
        jnp.float32
    )


def block_select(block_ids, first, count):
    columns = lax.iota(jnp.int32, count) + first
    return (block_ids.reshape(-1, 1) == columns.reshape(1, count)).astype(jnp.float32)


def reduce_range(coupling, tile_points, obs_point, first, count, per_turn, turn_count):

    def add_turn(turn, total):
        chosen = lax.dynamic_slice_in_dim(tile_points, turn * per_turn, per_turn, 0)
        local_ids = lax.dynamic_slice_in_dim(obs_point, turn * per_turn * TILE, per_turn * TILE, 0)
        values = lax.dynamic_slice_in_dim(coupling, turn * per_turn * TILE, per_turn * TILE, 1)
        inside = jnp.einsum(
            "rgt,gpt->rgp",
            values.reshape(3, per_turn, TILE),
            tile_onehot(local_ids, per_turn, PB),
            precision=lax.Precision.HIGHEST,
        )
        return total + jnp.einsum(
            "rgp,gb->rbp",
            inside,
            block_select(chosen, first, count),
            precision=lax.Precision.HIGHEST,
        )

    summed = lax.fori_loop(0, turn_count, add_turn, jnp.zeros((3, count, PB), jnp.float32))
    return summed.reshape(3, count * PB)


def on_device(
    cameras,
    increment,
    points,
    point_gradient,
    point_inverse,
    cam_jacobian,
    point_jacobian,
    observed,
    tile_block,
    tile_points,
    obs_camera,
    obs_point,
    accept,
):
    trial_cameras = cameras + increment
    group_trial, group_steps = side_by_side((trial_cameras, increment), "cam", 1, 0)
    every_trial, every_steps = side_by_side_2((group_trial, group_steps), PTS, 1, 0)
    stacked = jnp.concatenate([every_trial, every_steps], axis=0)
    cam_blocks = stacked.shape[1] // CB
    blocks = stacked.reshape(18, cam_blocks, CB)
    tile_count = tile_block.shape[0]
    obs_count = obs_camera.shape[0]
    per_turn = math.gcd(tile_count, 64)
    turn_count = tile_count // per_turn

    def lookup(turn, gathered):
        chosen = lax.dynamic_slice_in_dim(tile_block, turn * per_turn, per_turn, 0)
        cam_local = lax.dynamic_slice_in_dim(obs_camera, turn * per_turn * TILE, per_turn * TILE, 0)
        slabs = jnp.einsum(
            "rbc,gb->rgc",
            blocks,
            block_select(chosen, 0, cam_blocks),
            precision=lax.Precision.HIGHEST,
        )
        values = jnp.einsum(
            "rgc,gct->rgt",
            slabs,
            tile_onehot(cam_local, per_turn, CB),
            precision=lax.Precision.HIGHEST,
        )
        return lax.dynamic_update_slice_in_dim(
            gathered, values.reshape(18, per_turn * TILE), turn * per_turn * TILE, 1
        )

    per_obs = lax.fori_loop(0, turn_count, lookup, jnp.zeros((18, obs_count), jnp.float32))
    coupling = couple(cam_jacobian, point_jacobian, per_obs[9:18])
    point_count = points.shape[1]
    point_blocks = point_count // PB
    reduced = reduce_range(coupling, tile_points, obs_point, 0, point_blocks, per_turn, turn_count)
    summed = over_pieces(reduced, "cam")
    point_step = solve_points(point_inverse, point_gradient, summed)
    trial_blocks = (points + point_step).reshape(3, point_blocks, PB)

    def fetch(turn, gathered):
        chosen = lax.dynamic_slice_in_dim(tile_points, turn * per_turn, per_turn, 0)
        local_ids = lax.dynamic_slice_in_dim(obs_point, turn * per_turn * TILE, per_turn * TILE, 0)
        slabs = jnp.einsum(
            "rbp,gb->rgp",
            trial_blocks,
            block_select(chosen, 0, point_blocks),
            precision=lax.Precision.HIGHEST,
        )
        values = jnp.einsum(
            "rgp,gpt->rgt",
            slabs,
            tile_onehot(local_ids, per_turn, PB),
            precision=lax.Precision.HIGHEST,
        )
        return lax.dynamic_update_slice_in_dim(
            gathered, values.reshape(3, per_turn * TILE), turn * per_turn * TILE, 1
        )

    seen_points = lax.fori_loop(0, turn_count, fetch, jnp.zeros((3, obs_count), jnp.float32))
    residual = project(per_obs[0:9], seen_points) - observed
    cost_sum = one_axis_at_a_time(jnp.sum(residual * residual), PTS_CAM)
    obs_total = observed.shape[1] * lax.axis_size(PTS_CAM)
    trial_cost = cost_sum / (2.0 * obs_total)
    accepted_flag = jnp.remainder(accept, 2).astype(jnp.float32)
    return (
        residual,
        trial_cost,
        points + accepted_flag * point_step,
        cameras + accepted_flag * increment,
    )


def solution(mesh):
    split = Mesh(
        mesh.devices.reshape(4, 4, 2, mesh.shape["cam"]), ("pts_0", "pts_1", "pts_2", "cam")
    )
    in_specs = (
        P(None, PTS_CAM),
        P(None, PTS_CAM),
        P(None, PTS),
        P(None, PTS),
        P(None, PTS),
        P(None, PTS_CAM),
        P(None, PTS_CAM),
        P(None, PTS_CAM),
        P(PTS_CAM),
        P(PTS_CAM),
        P(PTS_CAM),
        P(PTS_CAM),
        P(),
    )
    out_specs = (P(None, PTS_CAM), P(), P(None, PTS), P(None, PTS_CAM))
    return jax.shard_map(
        on_device, mesh=split, in_specs=in_specs, out_specs=out_specs, check_vma=False
    )
```

profile of v0, /device:TPU:1, one launch (start us, length us, event | category | flops | bytes accessed | tf_op | source)
XLA Modules:
  0.0 705.0 jit_solution(1447611298619674717)
XLA Ops:
  9.8 11.3 %all_gather.6 = f32[18,512]{1,0:T(8,128)S(1)} all-gather(f32[18,128]{1,0:T(8,128)S(1)} %pad_maximum_fusion.2), channel_id=1, replica_groups=mesh['pts_0'=4,'pts_1'=4,'pts_2'=2,'cam'=4] {'cam'}, dimensions={1}, use_global_device_ids=true | all-gather | bytes 46080 | tf_op jit(solution)/shard_map/all_gather | solution.py:18
  22.5 10.4 %all-to-all-start = ((f32[32,18,512]{2,1,0:T(8,128)}), f32[32,18,512]{2,1,0:T(8,128)S(1)}, u32[]{:S(2)}, u32[]{:S(2)}) async-start(f32[32,18,512]{2,1,0:T(8,128)} %broadcast_in_dim.12), calls=%async_computation | async-start | bytes 3145728 | tf_op jit(solution)/shard_map/all_to_all | solution.py:33
  32.9 14.5 %convert_element_type.31 = f32[18,262144]{1,0:T(8,128)} convert(bf16[18,262144]{1,0:T(8,128)(2,1)} %param.25) | non-fusion elementwise | flops 4718592 | bytes 28311552 | tf_op jit(solution)/shard_map/convert_element_type | solution.py:85
  58.5 8.5 %broadcast_in_dim.11 = f32[18,262144]{1,0:T(8,128)} broadcast(f32[]{:T(128)} %constant.230.clone.1), dimensions={} | broadcast | bytes 18874372 | tf_op jit(solution)/shard_map/broadcast_in_dim | solution.py:184
  67.0 127.0 %while.46 = (s32[]{:T(128)}, f32[18,262144]{1,0:T(8,128)}, s32[262144]{0:T(1024)}, s32[1024]{0:T(1024)}, f32[18,128,128]{2,1,0:T(8,128)S(1)}, /*index=5*/s32[]{:...) while((s32[]{:T(128)}, f32[18,262144]{1,0:T(8,128)}, ...), condition=%wide.region_1.0_spmd, body=%wide.region_0.0_spmd.sunk | while | flops 681582592 | bytes 14877665 | solution.py:184
  193.9 20.6 %fusion.22 = (f32[262144]{0:T(1024)S(1)}, f32[262144]{0:T(1024)S(1)}) fusion(f32[18,262144]{1,0:T(8,128)} %convert_element_type.31, f32[18,262144]{1,0:T(8,128)} %get-tuple-element.401), kind=kLoop, calls=%fused_computation.33 | loop fusion | flops 8912896 | bytes 30408704 | tf_op jit(solution)/shard_map/reduce_sum | solution.py:87
  217.9 174.9 %while.48 = (s32[]{:T(128)}, f32[3,256,256]{2,1,0:T(8,128)S(1)}, s32[1024]{0:T(1024)}, s32[262144]{0:T(1024)}, f32[3,262144]{1,0:T(4,128)}, /*index=5*/s32[]{:T(...) while((s32[]{:T(128)}, f32[3,256,256]{2,1,0:T(8,128)S(1)}, ...), condition=%wide.region_6.0_spmd.clone, body=%wide.region_5.0_spmd.clone.sunk | while | flops 306593792 | bytes 2884575 | solution.py:135
  220.0 7.5 %fusion.86 = f32[3,64,256]{2,0,1:T(4,128)S(1)} fusion(f32[3,64,256]{2,0,1:T(4,128)S(1)} %bitcast.75, s32[64,256]{1,0:T(8,128)S(1)} %eq.443), kind=kOutput, calls=%fused_computation.24.clone.1 | convolution fusion | flops 155189248 | bytes 458752 | tf_op jit(solution)/shard_map/while/body/eval_jaxpr/rgt,gpt->rgp/dot_general | solution.py:122
  230.9 7.5 %fusion.86 = f32[3,64,256]{2,0,1:T(4,128)S(1)} fusion(f32[3,64,256]{2,0,1:T(4,128)S(1)} %bitcast.75, s32[64,256]{1,0:T(8,128)S(1)} %eq.443), kind=kOutput, calls=%fused_computation.24.clone.1 | convolution fusion | flops 155189248 | bytes 458752 | tf_op jit(solution)/shard_map/while/body/eval_jaxpr/rgt,gpt->rgp/dot_general | solution.py:122
  241.8 7.5 %fusion.86 = f32[3,64,256]{2,0,1:T(4,128)S(1)} fusion(f32[3,64,256]{2,0,1:T(4,128)S(1)} %bitcast.75, s32[64,256]{1,0:T(8,128)S(1)} %eq.443), kind=kOutput, calls=%fused_computation.24.clone.1 | convolution fusion | flops 155189248 | bytes 458752 | tf_op jit(solution)/shard_map/while/body/eval_jaxpr/rgt,gpt->rgp/dot_general | solution.py:122
  252.7 7.5 %fusion.86 = f32[3,64,256]{2,0,1:T(4,128)S(1)} fusion(f32[3,64,256]{2,0,1:T(4,128)S(1)} %bitcast.75, s32[64,256]{1,0:T(8,128)S(1)} %eq.443), kind=kOutput, calls=%fused_computation.24.clone.1 | convolution fusion | flops 155189248 | bytes 458752 | tf_op jit(solution)/shard_map/while/body/eval_jaxpr/rgt,gpt->rgp/dot_general | solution.py:122
  263.7 7.5 %fusion.86 = f32[3,64,256]{2,0,1:T(4,128)S(1)} fusion(f32[3,64,256]{2,0,1:T(4,128)S(1)} %bitcast.75, s32[64,256]{1,0:T(8,128)S(1)} %eq.443), kind=kOutput, calls=%fused_computation.24.clone.1 | convolution fusion | flops 155189248 | bytes 458752 | tf_op jit(solution)/shard_map/while/body/eval_jaxpr/rgt,gpt->rgp/dot_general | solution.py:122
  274.6 7.5 %fusion.86 = f32[3,64,256]{2,0,1:T(4,128)S(1)} fusion(f32[3,64,256]{2,0,1:T(4,128)S(1)} %bitcast.75, s32[64,256]{1,0:T(8,128)S(1)} %eq.443), kind=kOutput, calls=%fused_computation.24.clone.1 | convolution fusion | flops 155189248 | bytes 458752 | tf_op jit(solution)/shard_map/while/body/eval_jaxpr/rgt,gpt->rgp/dot_general | solution.py:122
  285.5 7.5 %fusion.86 = f32[3,64,256]{2,0,1:T(4,128)S(1)} fusion(f32[3,64,256]{2,0,1:T(4,128)S(1)} %bitcast.75, s32[64,256]{1,0:T(8,128)S(1)} %eq.443), kind=kOutput, calls=%fused_computation.24.clone.1 | convolution fusion | flops 155189248 | bytes 458752 | tf_op jit(solution)/shard_map/while/body/eval_jaxpr/rgt,gpt->rgp/dot_general | solution.py:122
  296.4 7.5 %fusion.86 = f32[3,64,256]{2,0,1:T(4,128)S(1)} fusion(f32[3,64,256]{2,0,1:T(4,128)S(1)} %bitcast.75, s32[64,256]{1,0:T(8,128)S(1)} %eq.443), kind=kOutput, calls=%fused_computation.24.clone.1 | convolution fusion | flops 155189248 | bytes 458752 | tf_op jit(solution)/shard_map/while/body/eval_jaxpr/rgt,gpt->rgp/dot_general | solution.py:122
  307.3 7.5 %fusion.86 = f32[3,64,256]{2,0,1:T(4,128)S(1)} fusion(f32[3,64,256]{2,0,1:T(4,128)S(1)} %bitcast.75, s32[64,256]{1,0:T(8,128)S(1)} %eq.443), kind=kOutput, calls=%fused_computation.24.clone.1 | convolution fusion | flops 155189248 | bytes 458752 | tf_op jit(solution)/shard_map/while/body/eval_jaxpr/rgt,gpt->rgp/dot_general | solution.py:122
  318.2 7.5 %fusion.86 = f32[3,64,256]{2,0,1:T(4,128)S(1)} fusion(f32[3,64,256]{2,0,1:T(4,128)S(1)} %bitcast.75, s32[64,256]{1,0:T(8,128)S(1)} %eq.443), kind=kOutput, calls=%fused_computation.24.clone.1 | convolution fusion | flops 155189248 | bytes 458752 | tf_op jit(solution)/shard_map/while/body/eval_jaxpr/rgt,gpt->rgp/dot_general | solution.py:122
  329.2 7.5 %fusion.86 = f32[3,64,256]{2,0,1:T(4,128)S(1)} fusion(f32[3,64,256]{2,0,1:T(4,128)S(1)} %bitcast.75, s32[64,256]{1,0:T(8,128)S(1)} %eq.443), kind=kOutput, calls=%fused_computation.24.clone.1 | convolution fusion | flops 155189248 | bytes 458752 | tf_op jit(solution)/shard_map/while/body/eval_jaxpr/rgt,gpt->rgp/dot_general | solution.py:122
  340.1 7.5 %fusion.86 = f32[3,64,256]{2,0,1:T(4,128)S(1)} fusion(f32[3,64,256]{2,0,1:T(4,128)S(1)} %bitcast.75, s32[64,256]{1,0:T(8,128)S(1)} %eq.443), kind=kOutput, calls=%fused_computation.24.clone.1 | convolution fusion | flops 155189248 | bytes 458752 | tf_op jit(solution)/shard_map/while/body/eval_jaxpr/rgt,gpt->rgp/dot_general | solution.py:122
  351.0 7.5 %fusion.86 = f32[3,64,256]{2,0,1:T(4,128)S(1)} fusion(f32[3,64,256]{2,0,1:T(4,128)S(1)} %bitcast.75, s32[64,256]{1,0:T(8,128)S(1)} %eq.443), kind=kOutput, calls=%fused_computation.24.clone.1 | convolution fusion | flops 155189248 | bytes 458752 | tf_op jit(solution)/shard_map/while/body/eval_jaxpr/rgt,gpt->rgp/dot_general | solution.py:122
  361.9 7.5 %fusion.86 = f32[3,64,256]{2,0,1:T(4,128)S(1)} fusion(f32[3,64,256]{2,0,1:T(4,128)S(1)} %bitcast.75, s32[64,256]{1,0:T(8,128)S(1)} %eq.443), kind=kOutput, calls=%fused_computation.24.clone.1 | convolution fusion | flops 155189248 | bytes 458752 | tf_op jit(solution)/shard_map/while/body/eval_jaxpr/rgt,gpt->rgp/dot_general | solution.py:122
  394.2 45.6 %all-gather.2.cloned.1.call-done = f32[4,3,65536]{2,1,0:T(4,128)} async-done(((f32[1,3,65536]{2,1,0:T(4,128)}), f32[4,3,65536]{2,1,0:T(4,128)}) %all-gather.2.cloned.1.call-update) | async-done | bytes 3145744 | tf_op jit(solution)/shard_map/all_gather | solution.py:50
  443.3 10.0 %multiply_add_fusion.5 = (f32[1,65536]{1,0:T(1,128)S(1)}, f32[1,65536]{1,0:T(1,128)S(1)}, f32[1,65536]{1,0:T(1,128)S(1)}) fusion(f32[9,65536]{1,0:T(8,128)} %param.24, f32[3,65536]{1,0:T(4,128)S(1)} %sub.24), kind=kLoop, calls=%fused_computation.112 | loop fusion | flops 983040 | bytes 3932160 | tf_op jit(solution)/shard_map/add | solution.py:96
  457.6 131.8 %while.47 = (s32[]{:T(128)}, f32[3,262144]{1,0:T(4,128)}, s32[262144]{0:T(1024)}, s32[1024]{0:T(1024)}, f32[3,256,256]{2,1,0:T(8,128)S(1)}, /*index=5*/s32[]{:T(...) while((s32[]{:T(128)}, f32[3,262144]{1,0:T(4,128)}, s32[262144]{0:T(1024)}, ...), condition=%wide.region_9.0_spmd, body=%wide.region_8.0_spmd.sunk | while | flops 306200576 | bytes 2163669 | solution.py:212
  589.4 13.8 %multiply_reduce_fusion.1 = (f32[262144]{0:T(1024)S(1)}, f32[262144]{0:T(1024)S(1)}) fusion(f32[18,262144]{1,0:T(8,128)} %get-tuple-element.401, f32[3,262144]{1,0:T(4,128)} %get-tuple-element.403), kind=kLoop, calls=%fused_computation.42 | loop fusion | flops 2621440 | bytes 8388608 | tf_op jit(solution)/shard_map/reduce_sum | solution.py:60
  603.2 16.8 %multiply_subtract_fusion.3 = (f32[1,262144]{1,0:T(1,128)S(1)}, f32[1,262144]{1,0:T(1,128)S(1)}, f32[1,262144]{1,0:T(1,128)S(1)}) fusion(f32[3,262144]{1,0:T(4,128)} %get-tuple-element.403, f32[18,262144]{1,0:T(8,128)} %get-tuple-element.401), kind=kLoop, calls=%fused_computation.106 | loop fusion | flops 2359296 | bytes 9437184 | tf_op jit(solution)/shard_map/sub | solution.py:66
  626.1 12.6 %fusion.26 = f32[3,262144]{1,0:T(4,128)S(1)} fusion(f32[1,262144]{1,0:T(1,128)S(1)} %get-tuple-element.462, f32[1,262144]{1,0:T(1,128)S(1)} %get-tuple-element.461, f32[1,262144]{1,0:T(1,128)S(1)} %get-tuple-element.460, f32[18,262144]{1,0:T(8,128)} %get-tuple-element.401, f32[3,262144]{1,0:T(4,128)} %get-tuple-element.403, ...), kind=kLoop, calls=%fused_computation.40 | loop fusion | flops 6291456 | bytes 18874368 | tf_op jit(solution)/shard_map/add | solution.py:76
  640.2 9.1 %multiply_reduce_fusion.3 = (f32[262144]{0:T(1024)S(1)}, f32[2,262144]{1,0:T(2,128)S(1)}) fusion(f32[262144]{0:T(1024)S(1)} %bitcast.79, f32[3,262144]{1,0:T(4,128)S(1)} %fusion.26), kind=kLoop, calls=%fused_computation.46 | loop fusion | flops 1310720 | bytes 6291456 | tf_op jit(solution)/shard_map/reduce_sum | solution.py:79
  649.4 9.9 %fusion.43 = f32[1,262144]{1,0:T(1,128)S(1)} fusion(f32[1,262144]{1,0:T(1,128)S(1)} %bitcast.77, f32[18,262144]{1,0:T(8,128)} %get-tuple-element.401), kind=kLoop, calls=%fused_computation.77 | loop fusion | flops 1572864 | bytes 5242880 | tf_op jit(solution)/shard_map/mul | solution.py:80
  663.3 9.0 %psum.28 = f32[]{:T(128)} all-reduce(f32[]{:T(128)} %get-tuple-element.456), channel_id=1, replica_groups=mesh['pts_0'=4,'pts_1'=4,'pts_2'=2,'cam'=4] {'pts_0'}, use_global_device_ids=true, to_apply=%region_13.15 | all-reduce | flops 1 | bytes 8 | tf_op jit(solution)/shard_map/psum | solution.py:55
  672.3 9.1 %psum.29 = f32[]{:T(128)} all-reduce(f32[]{:T(128)} %psum.28), channel_id=1, replica_groups=mesh['pts_0'=4,'pts_1'=4,'pts_2'=2,'cam'=4] {'pts_1'}, use_global_device_ids=true, to_apply=%region_14.16 | all-reduce | flops 1 | bytes 8 | tf_op jit(solution)/shard_map/psum | solution.py:55
  681.3 7.6 %psum.30 = f32[]{:T(128)} all-reduce(f32[]{:T(128)} %psum.29), channel_id=1, replica_groups=mesh['pts_0'=4,'pts_1'=4,'pts_2'=2,'cam'=4] {'pts_2'}, use_global_device_ids=true, to_apply=%region_15.17 | all-reduce | flops 1 | bytes 8 | tf_op jit(solution)/shard_map/psum | solution.py:55
  (360 shorter events, 372.2 us)
Async XLA Ops:
  22.5 33.0 %all-to-all-start = ((f32[32,18,512]{2,1,0:T(8,128)}), f32[32,18,512]{2,1,0:T(8,128)S(1)}, u32[]{:S(2)}, u32[]{:S(2)}) async-start(f32[32,18,512]{2,1,0:T(8,128)} %broadcast_in_dim.12), calls=%async_computation | async-start | bytes 3145728 | tf_op jit(solution)/shard_map/all_to_all | solution.py:33
  32.9 406.9 %all-gather.2.cloned.1.call-start = ((), (), s32[]{:S(2)}) async-start(), calls=%async_computation.1 | async-start | bytes 5242880 | tf_op jit(solution)/shard_map/all_gather | solution.py:50
  32.9 14.5 %copy-start = (bf16[6,262144]{1,0:T(8,128)(2,1)S(1)}, bf16[6,262144]{1,0:T(8,128)(2,1)}, u32[]{:S(2)}) copy-start(bf16[6,262144]{1,0:T(8,128)(2,1)} %param.26) | copy-start | bytes 9437188
  193.9 20.6 %slice-start = ((s8[8388608]{0:T(1024)(128)(4,1)}), s8[4194304]{0:T(1024)(128)(4,1)S(1)}, s32[]{:S(2)}) async-start(s8[8388608]{0:T(1024)(128)(4,1)} %bitcast.71), calls=%async_computation.2 | async-start | bytes 8388608
  193.9 20.6 %slice-start.1 = ((s8[8388608]{0:T(1024)(128)(4,1)}), s8[4194304]{0:T(1024)(128)(4,1)S(1)}, s32[]{:S(2)}) async-start(s8[8388608]{0:T(1024)(128)(4,1)} %bitcast.71), calls=%async_computation.3 | async-start | bytes 8388608
  392.8 50.2 %copy-start.2 = (f32[3,65536]{1,0:T(4,128)S(1)}, f32[3,65536]{1,0:T(4,128)}, u32[]{:S(2)}) copy-start(f32[3,65536]{1,0:T(4,128)} %param.23) | copy-start | bytes 2359300
  443.0 10.4 %copy-start.3 = (f32[3,65536]{1,0:T(4,128)S(1)}, f32[3,65536]{1,0:T(4,128)}, u32[]{:S(2)}) copy-start(f32[3,65536]{1,0:T(4,128)} %param.22) | copy-start | bytes 2359300
  649.4 9.9 %copy-start.1 = (f32[2,262144]{1,0:T(2,128)S(1)}, f32[2,262144]{1,0:T(2,128)}, u32[]{:S(2)}) copy-start(f32[2,262144]{1,0:T(2,128)} %param.27) | copy-start | bytes 6291460
Sparse Core Ops, SparseCore 0:
  394.3 45.4 all-gather.1
where the time goes:
time: 719 us; the launch traced here: 705 us
  matrix products  281 us (39%)
  local copies, waits for them, and re-layouts  165 us (23%)
  other arithmetic  134 us (19%)
  waiting for transfers between devices  50.2 us (7%)
  blocking collectives  44.2 us (6%)
  between operations  16.9 us (2%)
  starting transfers between devices  10.4 us (1%)
    dot_general x16, matrix products, add_turn(): jnp.einsum('rgt,gpt->rgp', values.reshape(3, per_turn, TILE), tile_onehot...  120 us
    dot_general x16, matrix products, fetch(): jnp.einsum('rgp,gpt->rgt', slabs, tile_onehot(local_ids, per_turn, PB), p...  85.7 us
    dot_general x16, matrix products, lookup(): jnp.einsum('rgc,gct->rgt', slabs, tile_onehot(cam_local, per_turn, CB), p...  47.6 us
    all_gather x1, waiting for transfers between devices, over_pieces(): return lax.all_gather(array, axis).sum(0)  45.6 us
    psum x4, blocking collectives, one_axis_at_a_time(): array = lax.psum(array, axis)  32.9 us
    reduce_sum x1, other arithmetic, couple(): first_row = jnp.sum(cam_rows[0:9] * cam_steps, axis=0)  20.6 us
    dynamic_update_slice x16, local copies, waits for them, and re-layouts, lookup(): lax.dynamic_update_slice_in_dim(gathered, values.reshape(18, per_turn * T...  19.8 us
    while x32, local copies, waits for them, and re-layouts  17.5 us
  transfers between devices with their start and end apart: 2, of which 2 were waited for; matrix products, arithmetic and copies ran while one was open for 3% of the time, Pallas kernels for 0%

commit v1 on v0

v1 whole, which is shorter than its diff:
```python
import functools, math
import jax, jax.numpy as jnp
from jax import lax
from jax.experimental import pallas as pl
from jax.experimental.pallas import tpu as pltpu
from jax.sharding import Mesh
from jax.sharding import PartitionSpec as P

CB=128; PB=256; TILE=256
F32=jnp.float32
GROUP=1024
TPG=GROUP//TILE

def lane_gather(table, index):
    return lax.gather(table, index[..., None],
        lax.GatherDimensionNumbers(offset_dims=(), collapsed_slice_dims=(1,), start_index_map=(1,),
            operand_batching_dims=(0,), start_indices_batching_dims=(0,)),
        slice_sizes=(1,1), mode=lax.GatherScatterMode.PROMISE_IN_BOUNDS)

def tile_rows(rows, row_id):
    a,b,c,d = rows
    return jnp.where(row_id<4, jnp.where(row_id<2,a,b), jnp.where(row_id<6,c,d))

def spread(ref, first):
    return ref[pl.ds(first, 8, stride=0), :]

PH=8; PL=32

def reduce_body(chunk, blocks_n, tb, tp, inc_ref, cj_ref, pj_ref, oc_ref, op_ref, out_ref, acc, jscr, pscr, wscr):
    step = pl.program_id(0)
    groups = chunk//GROUP
    row_id = lax.broadcasted_iota(jnp.int32,(8,128),0)
    @pl.when(step==0)
    def _():
        def zero(i,_):
            acc[pl.ds(pl.multiple_of(i*64,64),64),:] = jnp.zeros((64,PL),F32)
            return 0
        lax.fori_loop(0, blocks_n, zero, 0)
        wscr[...] = jnp.zeros_like(wscr)
    def couple(g, slot):
        base = step*(chunk//TILE) + g*TPG
        cams = [tb[base+i]*9 for i in range(TPG)]
        cam = oc_ref[pl.ds(pl.multiple_of(g*8,8),8),:]
        for j in range(8):
            at = pl.ds(pl.multiple_of(g*GROUP+j*128,128),128)
            jscr[slot, j*24:j*24+18,:] = cj_ref[:,at].astype(F32)
            pscr[slot, j*8:j*8+6,:] = pj_ref[:,at].astype(F32)
        first=second=None
        for m in range(9):
            t = tile_rows([spread(inc_ref, c+m) for c in cams], row_id)
            v = lane_gather(t, cam)
            a = jscr[slot, pl.ds(m,8,stride=24),:]*v
            b = jscr[slot, pl.ds(9+m,8,stride=24),:]*v
            first = a if first is None else first+a
            second = b if second is None else second+b
        for n in range(3):
            v = pscr[slot, pl.ds(n,8,stride=8),:]*first + pscr[slot, pl.ds(3+n,8,stride=8),:]*second
            hi = v.astype(jnp.bfloat16).astype(F32)
            wscr[slot, pl.ds(n,8,stride=8),:] = hi
            wscr[slot, pl.ds(3+n,8,stride=8),:] = v-hi
    def scatter(g, slot):
        base = step*(chunk//TILE) + g*TPG
        for t in range(TPG):
            lhs=[]; rhs=[]
            for h in range(2):
                s=2*t+h
                w = wscr[slot, s*8:s*8+8,:]
                ids = op_ref[pl.ds(g*8+s,8,stride=0),:]
                hi = lax.shift_right_logical(ids,5)
                lo = ids & 31
                lhs.append(jnp.concatenate([jnp.where(hi==k,w,0.0) for k in range(PH)],axis=0).astype(jnp.bfloat16))
                rhs.append(jnp.concatenate([jnp.where(lo-8*k==row_id,1.0,0.0) for k in range(PL//8)],axis=0).astype(jnp.bfloat16))
            L=jnp.concatenate(lhs,axis=1); R=jnp.concatenate(rhs,axis=1)
            r = lax.dot_general(L,R,(((1,),(1,)),((),())),preferred_element_type=F32)
            at = pl.ds(pl.multiple_of(tp[base+t]*64,64),64)
            acc[at,:] += r
    UN=2
    def body(i,_):
        for u in range(UN):
            couple(i*UN+u, u)
            scatter(i*UN+u, u)
        return 0
    lax.fori_loop(0, groups//UN, body, 0)
    @pl.when(step==pl.num_programs(0)-1)
    def _():
        def flush(i,_):
            for h in range(2):
                parts=[]
                for k in range(4):
                    x = acc[pl.ds(pl.multiple_of(i*64+h*32+k*8,8),8),:]
                    parts.append(x)
                x=jnp.concatenate(parts,axis=1)
                s = x[0:3,:]+x[3:6,:]
                out_ref[:, pl.ds(pl.multiple_of(i*PB+h*128,128),128)] = s
            return 0
        lax.fori_loop(0, blocks_n, flush, 0)

def reduce_points(inc, cj, pj, oc, op, tb, tp, npts, chunk=8192):
    n=cj.shape[1]
    blocks_n=npts//PB
    return pl.pallas_call(
        functools.partial(reduce_body, chunk, blocks_n),
        out_shape=jax.ShapeDtypeStruct((3,npts),F32),
        grid_spec=pltpu.PrefetchScalarGridSpec(
            num_scalar_prefetch=2, grid=(n//chunk,),
            in_specs=[
                pl.BlockSpec(inc.shape, lambda i,*_:(0,0)),
                pl.BlockSpec((18,chunk), lambda i,*_:(0,i)),
                pl.BlockSpec((6,chunk), lambda i,*_:(0,i)),
                pl.BlockSpec((chunk//128,128), lambda i,*_:(i,0)),
                pl.BlockSpec((chunk//128,128), lambda i,*_:(i,0)),
            ],
            out_specs=pl.BlockSpec((3,npts), lambda i,*_:(0,0)),
            scratch_shapes=[pltpu.VMEM((blocks_n*64,PL),F32), pltpu.VMEM((2,192,128),F32), pltpu.VMEM((2,64,128),F32), pltpu.VMEM((2,64,128),F32)],
        ),
        compiler_params=pltpu.CompilerParams(dimension_semantics=("arbitrary",), vmem_limit_bytes=48*1024*1024),
        name="reduce_points",
    )(tb,tp,inc,cj,pj,oc,op)

CT=10
def project_body(chunk, tb, tp, cam_ref, pts_ref, oc_ref, op_ref, ob_ref, res_ref, cost_ref):
    step=pl.program_id(0)
    groups=chunk//GROUP
    row_id=lax.broadcasted_iota(jnp.int32,(8,128),0)
    @pl.when(step==0)
    def _():
        cost_ref[...]=jnp.zeros_like(cost_ref)
    def one(g):
        base=step*(chunk//TILE)+g*TPG
        cams=[tb[base+i]*CT for i in range(TPG)]
        pts=[tp[base+i]*8 for i in range(TPG)]
        at8=pl.ds(pl.multiple_of(g*8,8),8)
        cam=oc_ref[at8,:]; pid=op_ref[at8,:]
        upper=pid>=128; plow=pid&127
        def look(r): return lane_gather(tile_rows([spread(cam_ref,c+r) for c in cams],row_id),cam)
        def lookp(r):
            a=lane_gather(tile_rows([spread(pts_ref,p+r) for p in pts],row_id),plow)
            b=lane_gather(tile_rows([spread(pts_ref,p+4+r) for p in pts],row_id),plow)
            return jnp.where(upper,b,a)
        x,y,z=lookp(0),lookp(1),lookp(2)
        vx,vy,vz,r,t0,t1,t2,f0,f1,f2=[look(i) for i in range(CT)]
        ax=vy*z-vz*y; ay=vz*x-vx*z; az=vx*y-vy*x
        px=x+r*ax+(vy*az-vz*ay)+t0
        py=y+r*ay+(vz*ax-vx*az)+t1
        pz=z+r*az+(vx*ay-vy*ax)+t2
        inv=1.0/jnp.maximum(-pz,1.0)
        u=px*inv; v=py*inv
        q=u*u+v*v
        fac=f0+q*(f1+q*f2)
        o0=pl.ds(g*16,8,stride=2); o1=pl.ds(g*16+1,8,stride=2)
        ru=fac*u-ob_ref[o0,:]; rv=fac*v-ob_ref[o1,:]
        res_ref[o0,:]=ru; res_ref[o1,:]=rv
        return ru*ru+rv*rv
    UN=2
    def body(i,c):
        for u in range(UN): c=c+one(i*UN+u)
        return c
    cost_ref[...]+=lax.fori_loop(0,groups//UN,body,jnp.zeros((8,128),F32))

def project_points(cam, pts, oc, op, ob, tb, tp, chunk=8192):
    n=oc.shape[0]*128
    return pl.pallas_call(
        functools.partial(project_body, chunk),
        out_shape=(jax.ShapeDtypeStruct((n//64,128),F32), jax.ShapeDtypeStruct((8,128),F32)),
        grid_spec=pltpu.PrefetchScalarGridSpec(
            num_scalar_prefetch=2, grid=(n//chunk,),
            in_specs=[
                pl.BlockSpec(cam.shape, lambda i,*_:(0,0)),
                pl.BlockSpec(pts.shape, lambda i,*_:(0,0)),
                pl.BlockSpec((chunk//128,128), lambda i,*_:(i,0)),
                pl.BlockSpec((chunk//128,128), lambda i,*_:(i,0)),
                pl.BlockSpec((chunk//64,128), lambda i,*_:(i,0)),
            ],
            out_specs=(pl.BlockSpec((chunk//64,128), lambda i,*_:(i,0)), pl.BlockSpec((8,128), lambda i,*_:(0,0))),
        ),
        compiler_params=pltpu.CompilerParams(dimension_semantics=("arbitrary",), vmem_limit_bytes=32*1024*1024),
        name="project_points",
    )(tb,tp,cam,pts,oc,op,ob)


CAM = "cam"
PTS = ("pts_0", "pts_1", "pts_2")
PTS_CAM = PTS + (CAM,)
RT2 = math.sqrt(2.0)


def camera_rows(trial):
    w = trial[0:3]
    half = 0.5 * jnp.sqrt(jnp.sum(w * w, axis=0, keepdims=True))
    v = (0.5 * RT2) * jnp.sinc(half / math.pi) * w
    r = RT2 * jnp.cos(half)
    f = trial[6:7]
    return jnp.concatenate([v, r, trial[3:6], f, f * trial[7:8], f * trial[8:9]], axis=0)


def rows_of(x):
    n = x.shape[1] // 128
    return x.reshape(x.shape[0], n, 128).transpose(1, 0, 2).reshape(n * x.shape[0], 128)


def on_device(cameras, increment, points, gradient, inverse, cj, pj, observed, tb, tp, oc, op, accept):
    trial = cameras + increment
    inc_tab = lax.all_gather(increment, PTS_CAM, axis=0, tiled=True)
    cam_tab = lax.all_gather(camera_rows(trial), PTS_CAM, axis=0, tiled=True)
    oc2 = oc.reshape(-1, 128)
    op2 = op.reshape(-1, 128)
    reduced = reduce_points(inc_tab, cj, pj, oc2, op2, tb, tp, points.shape[1])
    reduced = lax.psum(reduced, CAM)
    d = gradient - reduced
    step = jnp.stack([inverse[3*i]*d[0] + inverse[3*i+1]*d[1] + inverse[3*i+2]*d[2] for i in range(3)])
    new = points + step
    pts_tab = rows_of(jnp.concatenate([new, jnp.zeros_like(new[0:1])], axis=0))
    res, cost = project_points(cam_tab, pts_tab, oc2, op2, rows_of(observed), tb, tp)
    n = observed.shape[1]
    residual = res.reshape(n // 128, 2, 128).transpose(1, 0, 2).reshape(2, n)
    total = lax.psum(jnp.sum(cost), PTS_CAM)
    flag = jnp.remainder(accept, 2).astype(F32)
    return (residual, total / (2.0 * n * lax.axis_size(PTS_CAM)), points + flag * step, cameras + flag * increment)


def solution(mesh):
    split = Mesh(mesh.devices.reshape(4, 4, 2, mesh.shape["cam"]), PTS_CAM)
    in_specs = (P(None, PTS_CAM), P(None, PTS_CAM), P(None, PTS), P(None, PTS), P(None, PTS),
                P(None, PTS_CAM), P(None, PTS_CAM), P(None, PTS_CAM),
                P(PTS_CAM), P(PTS_CAM), P(PTS_CAM), P(PTS_CAM), P())
    out_specs = (P(None, PTS_CAM), P(), P(None, PTS), P(None, PTS_CAM))
    return jax.shard_map(on_device, mesh=split, in_specs=in_specs, out_specs=out_specs, check_vma=False)
```

time: 719 us -> 310 us (0.43); the launches traced: 705 us -> 310 us
  matrix products: 281 us -> 0 us
  local copies, waits for them, and re-layouts: 165 us -> 4.23 us
  blocking collectives: 44.2 us -> 191 us
  other arithmetic: 134 us -> 14.7 us
  Pallas kernels: 0 us -> 83.6 us
  waiting for transfers between devices: 50.2 us -> 0.04 us
  starting transfers between devices: 10.4 us -> 0.04 us
    dot_general x96 -> x0, matrix products: 281 us -> none  [the longest x16 120 us: add_turn(): jnp.einsum('rgt,gpt->rgp', values.reshape(3, per_turn, TILE), tile_onehot...]
    all_gather x1 -> x2, blocking collectives: 11.3 us -> 125 us  [the longest x1 64.1 us: on_device(): inc_tab = lax.all_gather(increment, PTS_CAM, axis=0, tiled=True)]
    dynamic_slice x112 -> x0, local copies, waits for them, and re-layouts: 93.5 us -> none  [the longest x16 16 us: add_turn(): lax.dynamic_slice_in_dim(coupling, turn * per_turn * TILE, per_turn * TIL...]
    pallas_call x0 -> x2, Pallas kernels: none -> 83.6 us  [the longest x1 63.5 us: reduce_points(): pl.pallas_call(functools.partial(reduce_body, chunk, blocks_n), out_shape...]
    reduce_sum x5 -> x2, other arithmetic: 50.6 us -> 0.62 us  [the longest x1 0.6 us: on_device(): total = lax.psum(jnp.sum(cost), PTS_CAM)]
    all_gather x1 -> x0, waiting for transfers between devices: 45.6 us -> none  [over_pieces(): return lax.all_gather(array, axis).sum(0)]
    psum x4 -> x1, blocking collectives: 32.9 us -> 65.2 us  [on_device(): total = lax.psum(jnp.sum(cost), PTS_CAM)]
    dynamic_update_slice x32 -> x0, local copies, waits for them, and re-layouts: 32.1 us -> none  [the longest x16 19.8 us: lookup(): lax.dynamic_update_slice_in_dim(gathered, values.reshape(18, per_turn * T...]
  transfers between devices with their start and end apart: 2 -> 1, of which waited for: 2 -> 0; matrix products, arithmetic and copies ran while one was open for 3% -> 0% of each run, Pallas kernels for 0% -> 0%
where the time goes in v1:
time: 310 us
  blocking collectives  191 us (62%)
  Pallas kernels  83.6 us (27%)
  between operations  16.7 us (5%)
  other arithmetic  14.7 us (5%)
  local copies, waits for them, and re-layouts  4.23 us (1%)
    psum x1, blocking collectives, on_device(): total = lax.psum(jnp.sum(cost), PTS_CAM)  65.2 us
    all_gather x1, blocking collectives, on_device(): inc_tab = lax.all_gather(increment, PTS_CAM, axis=0, tiled=True)  64.1 us
    pallas_call x1, Pallas kernels, reduce_points(): pl.pallas_call(functools.partial(reduce_body, chunk, blocks_n), out_shape...  63.5 us
    all_gather x1, blocking collectives, on_device(): cam_tab = lax.all_gather(camera_rows(trial), PTS_CAM, axis=0, tiled=True)  61.2 us
    pallas_call x1, Pallas kernels, project_points(): pl.pallas_call(functools.partial(project_body, chunk), out_shape=(jax.Sha...  20.1 us
    add x1, other arithmetic, on_device(): inverse[3 * i] * d[0] + inverse[3 * i + 1] * d[1]  9.97 us
  transfers between devices with their start and end apart: 1, of which 0 were waited for; matrix products, arithmetic and copies ran while one was open for 0% of the time, Pallas kernels for 0%

profile of v1, /device:TPU:1, one launch (start us, length us, event | category | flops | bytes accessed | tf_op | source)
XLA Modules:
  0.0 309.9 jit_solution(9024256296743230582)
XLA Ops:
  7.2 0.0 all-reduce.3.cloned.1.call-start
  7.2 64.1 %all-gather.1 = f32[128,9,128]{2,1,0:T(8,128)S(1)} all-gather(f32[1,9,128]{2,1,0:T(8,128)} %bitcast.28), channel_id=1, replica_groups=mesh['pts_0'=4,'pts_1'=4,'pts_2'=2,'cam'=4] {'pts_0','pts_1','pts_2','cam'}, dimensions={0}, use_global_device_ids=true | all-gather | bytes 594432 | tf_op jit(solution)/shard_map/all_gather | solution.py:203
  71.3 0.1 reshape.141.inc_ref
  71.4 0.0 copy-start
  71.4 1.2 copy-done
  72.6 1.2 copy-done.2
  73.8 0.7 copy-done.5
  74.5 0.7 copy-done.7
  75.2 63.5 %reduce_points.1 = f32[3,65536]{1,0:T(4,128)} custom-call(s32[1024]{0:T(1024)S(1)} %copy-done.5, s32[1024]{0:T(1024)S(1)} %copy-done.7, f32[1152,128]{1,0:T(8,128)S(1)} %reshape.141.inc_ref, bf16[18,262144]{1,0:T(8,128)(2,1)} %cj_ref.1, bf16[6,262144]{1,0:T(8,128)(2,1)} %pj_ref.1, s32[2048,128]{1,0:T(8,128)S(1)} %bitcast.21, s32[2048,128]{1,0:T(8,128)S(1)} %bitcast.23), custom_call_target="tpu_custom_call" | custom-call | tf_op jit(solution)/shard_map/reduce_points/pallas_call | solution.py:101
  138.7 0.0 all-reduce.3.cloned.1.call-update
  139.4 0.0 copy-done.11
  139.5 0.0 copy-done.12
  139.5 0.6 multiply_add_fusion.4
  140.2 61.2 %all-gather = f32[128,10,128]{2,1,0:T(8,128)S(1)} all-gather(f32[1,10,128]{2,1,0:T(8,128)S(1)} %bitcast.27), channel_id=1, replica_groups=mesh['pts_0'=4,'pts_1'=4,'pts_2'=2,'cam'=4] {'pts_0','pts_1','pts_2','cam'}, dimensions={0}, use_global_device_ids=true | all-gather | bytes 660480 | tf_op jit(solution)/shard_map/all_gather | solution.py:204
  201.5 0.1 reshape.139.cam_ref
  201.5 0.0 copy-start.10
  201.5 0.0 all-reduce.3.cloned.1.call-done
  201.6 1.6 sub.23
  203.2 0.0 copy-start.1
  203.2 0.0 copy-start.3
  203.2 0.0 copy-start.4
  203.2 0.0 copy-start.6
  203.2 0.0 copy-start.8
  203.2 10.0 %multiply_add_fusion.3 = (f32[1,65536]{1,0:T(1,128)S(1)}, f32[1,65536]{1,0:T(1,128)S(1)}, f32[1,65536]{1,0:T(1,128)S(1)}) fusion(f32[9,65536]{1,0:T(8,128)} %param.17, f32[3,65536]{1,0:T(4,128)S(1)} %sub.23), kind=kLoop, calls=%fused_computation.5 | loop fusion | flops 983040 | bytes 3932160 | tf_op jit(solution)/shard_map/add | solution.py:210
  213.2 0.0 copy-done.10
  213.2 1.9 multiply_add_fusion
  215.1 0.2 concatenate.8
  215.3 0.0 copy-done.1
  215.3 0.0 copy-done.3
  215.3 20.1 %project_points.1 = (f32[4096,128]{1,0:T(8,128)}, f32[8,128]{1,0:T(8,128)S(1)}) custom-call(s32[1024]{0:T(1024)S(1)} %copy-done.6, s32[1024]{0:T(1024)S(1)} %copy-done.8, f32[1280,128]{1,0:T(8,128)S(1)} %reshape.139.cam_ref, f32[2048,128]{1,0:T(8,128)S(1)} %bitcast.25, s32[2048,128]{1,0:T(8,128)S(1)} %bitcast.22, s32[2048,128]{1,0:T(8,128)S(1)} %bitcast.24, ...), custom_call_target="tpu_custom_call" | custom-call | tf_op jit(solution)/shard_map/project_points/pallas_call | solution.py:162
  235.4 0.6 reduce_sum.19
  236.0 65.2 %psum.15 = f32[]{:T(128)} all-reduce(f32[]{:T(128)} %reduce_sum.19), channel_id=1, replica_groups=mesh['pts_0'=4,'pts_1'=4,'pts_2'=2,'cam'=4] {'pts_0','pts_1','pts_2','cam'}, use_global_device_ids=true, to_apply=%region_3.4 | all-reduce | flops 1 | bytes 8 | tf_op jit(solution)/shard_map/psum | solution.py:216
  (16 shorter events, 0.1 us)
Async XLA Ops:
  7.2 194.4 %all-reduce.3.cloned.1.call-start = ((), (), s32[]{:S(2)}) async-start(), calls=%async_computation | async-start | bytes 2097152 | tf_op jit(solution)/shard_map/psum | solution.py:208
  71.4 1.2 copy-start
  72.6 1.2 copy-start.2
  73.8 0.7 copy-start.5
  74.5 0.7 copy-start.7
  75.2 64.2 %copy-start.11 = (f32[9,128]{1,0:T(8,128)S(1)}, f32[9,128]{1,0:T(8,128)}, u32[]{:S(2)}) copy-start(f32[9,128]{1,0:T(8,128)} %param.14) | copy-start | bytes 13828
  75.2 64.2 %copy-start.12 = (f32[9,128]{1,0:T(8,128)S(1)}, f32[9,128]{1,0:T(8,128)}, u32[]{:S(2)}) copy-start(f32[9,128]{1,0:T(8,128)} %param.13) | copy-start | bytes 13828
  138.7 62.9 %copy-start.9 = (f32[3,65536]{1,0:T(4,128)S(1)}, f32[3,65536]{1,0:T(4,128)}, u32[]{:S(2)}) copy-start(f32[3,65536]{1,0:T(4,128)} %param.16) | copy-start | bytes 2359300
  201.5 11.7 %copy-start.10 = (f32[3,65536]{1,0:T(4,128)S(1)}, f32[3,65536]{1,0:T(4,128)}, u32[]{:S(2)}) copy-start(f32[3,65536]{1,0:T(4,128)} %param.15) | copy-start | bytes 2359300
  203.2 12.1 %copy-start.1 = (s32[262144]{0:T(1024)S(1)}, s32[262144]{0:T(1024)}, u32[]{:S(2)}) copy-start(s32[262144]{0:T(1024)} %param.23) | copy-start | bytes 3145732
  203.2 12.1 %copy-start.3 = (s32[262144]{0:T(1024)S(1)}, s32[262144]{0:T(1024)}, u32[]{:S(2)}) copy-start(s32[262144]{0:T(1024)} %param.24) | copy-start | bytes 3145732
  203.2 12.1 %copy-start.4 = (f32[2,262144]{1,0:T(2,128)S(1)}, f32[2,262144]{1,0:T(2,128)}, u32[]{:S(2)}) copy-start(f32[2,262144]{1,0:T(2,128)} %param.20) | copy-start | bytes 6291460
  203.2 12.1 %copy-start.6 = (s32[1024]{0:T(1024)S(1)}, s32[1024]{0:T(1024)}, u32[]{:S(2)}) copy-start(s32[1024]{0:T(1024)} %tb.3) | copy-start | bytes 12292
  203.2 12.1 %copy-start.8 = (s32[1024]{0:T(1024)S(1)}, s32[1024]{0:T(1024)}, u32[]{:S(2)}) copy-start(s32[1024]{0:T(1024)} %tp.3) | copy-start | bytes 12292
Sparse Core Ops, SparseCore 0:
  138.8 42.9 all-reduce.2

commit v2 on v1

v2 whole, which is shorter than its diff:
```python
import functools, math
import jax, jax.numpy as jnp
from jax import lax
from jax.experimental import pallas as pl
from jax.experimental.pallas import tpu as pltpu
from jax.sharding import Mesh
from jax.sharding import PartitionSpec as P

CB=128; PB=256; TILE=256
F32=jnp.float32
GROUP=1024
TPG=GROUP//TILE

def lane_gather(table, index):
    return lax.gather(table, index[..., None],
        lax.GatherDimensionNumbers(offset_dims=(), collapsed_slice_dims=(1,), start_index_map=(1,),
            operand_batching_dims=(0,), start_indices_batching_dims=(0,)),
        slice_sizes=(1,1), mode=lax.GatherScatterMode.PROMISE_IN_BOUNDS)

def tile_rows(rows, row_id):
    a,b,c,d = rows
    return jnp.where(row_id<4, jnp.where(row_id<2,a,b), jnp.where(row_id<6,c,d))

def spread(ref, first):
    return ref[pl.ds(first, 8, stride=0), :]

PH=8; PL=32
UN=8

def reduce_body(chunk, blocks_n, tb, tp, word, inc_ref, cj_ref, pj_ref, oc_ref, op_ref, cam_ref, own_ref, out_ref, kept_ref, acc, jscr, pscr, wscr):
    step = pl.program_id(0)
    groups = chunk//GROUP
    row_id = lax.broadcasted_iota(jnp.int32,(8,128),0)
    @pl.when(step==0)
    def _():
        def zero(i,_):
            acc[pl.ds(pl.multiple_of(i*(PH*8),PH*8),PH*8),:] = jnp.zeros((PH*8,PL),F32)
            return 0
        lax.fori_loop(0, blocks_n, zero, 0, unroll=8)
        wscr[...] = jnp.zeros_like(wscr)
        kept_ref[...] = cam_ref[...] + (word[0] & 1).astype(F32)*own_ref[...]
    def couple(g, slot):
        base = step*(chunk//TILE) + g*TPG
        cams = [tb[base+i]*9 for i in range(TPG)]
        cam = oc_ref[pl.ds(pl.multiple_of(g*8,8),8),:]
        for j in range(8):
            at = pl.ds(pl.multiple_of(g*GROUP+j*128,128),128)
            jscr[slot, j*24:j*24+18,:] = cj_ref[:,at].astype(F32)
            pscr[slot, j*8:j*8+6,:] = pj_ref[:,at].astype(F32)
        first=second=None
        for m in range(9):
            t = tile_rows([spread(inc_ref, c+m) for c in cams], row_id)
            v = lane_gather(t, cam)
            a = jscr[slot, pl.ds(m,8,stride=24),:]*v
            b = jscr[slot, pl.ds(9+m,8,stride=24),:]*v
            first = a if first is None else first+a
            second = b if second is None else second+b
        for n in range(3):
            v = pscr[slot, pl.ds(n,8,stride=8),:]*first + pscr[slot, pl.ds(3+n,8,stride=8),:]*second
            hi = v.astype(jnp.bfloat16).astype(F32)
            wscr[slot, pl.ds(n,8,stride=8),:] = hi
            wscr[slot, pl.ds(3+n,8,stride=8),:] = v-hi
    def scatter(g, slot):
        base = step*(chunk//TILE) + g*TPG
        for t in range(TPG):
            lhs=[]; rhs=[]
            for h in range(2):
                s=2*t+h
                w = wscr[slot, s*8:s*8+8,:]
                ids = op_ref[pl.ds(g*8+s,8,stride=0),:]
                hi = lax.shift_right_logical(ids,PL.bit_length()-1)
                lo = ids & (PL-1)
                lhs.append(jnp.concatenate([jnp.where(hi==k,w,0.0) for k in range(PH)],axis=0).astype(jnp.bfloat16))
                rhs.append(jnp.concatenate([jnp.where(lo-8*k==row_id,1.0,0.0) for k in range(PL//8)],axis=0).astype(jnp.bfloat16))
            L=jnp.concatenate(lhs,axis=1); R=jnp.concatenate(rhs,axis=1)
            r = lax.dot_general(L,R,(((1,),(1,)),((),())),preferred_element_type=F32)
            at = pl.ds(pl.multiple_of(tp[base+t]*(PH*8),PH*8),PH*8)
            acc[at,:] += r
    def body(i,_):
        for u in range(UN): couple(i*UN+u, u)
        for u in range(UN): scatter(i*UN+u, u)
        return 0
    lax.fori_loop(0, groups//UN, body, 0)
    @pl.when(step==pl.num_programs(0)-1)
    def _():
        def flush(i,_):
            for h in range(2):
                n = 128//PL
                x = jnp.concatenate([acc[pl.ds(pl.multiple_of(i*(PH*8)+(h*n+k)*8,8),8),:] for k in range(n)],axis=1)
                s = x[0:3,:]+x[3:6,:]
                for n in range(3):
                    out_ref[n, pl.ds(2*i+h,1),:] = s[n:n+1,:]
            return 0
        lax.fori_loop(0, blocks_n, flush, 0, unroll=8)

def reduce_points(inc, cj, pj, oc, op, tb, tp, word, cameras, increment, npts, chunk=32768):
    n=cj.shape[1]
    blocks_n=npts//PB
    return pl.pallas_call(
        functools.partial(reduce_body, chunk, blocks_n),
        out_shape=(jax.ShapeDtypeStruct((3,npts//128,128),F32), jax.ShapeDtypeStruct((9,128),F32)),
        grid_spec=pltpu.PrefetchScalarGridSpec(
            num_scalar_prefetch=3, grid=(n//chunk,),
            in_specs=[
                pl.BlockSpec(inc.shape, lambda i,*_:(0,0)),
                pl.BlockSpec((18,chunk), lambda i,*_:(0,i)),
                pl.BlockSpec((6,chunk), lambda i,*_:(0,i)),
                pl.BlockSpec((chunk//128,128), lambda i,*_:(i,0)),
                pl.BlockSpec((chunk//128,128), lambda i,*_:(i,0)),
                pl.BlockSpec((9,128), lambda i,*_:(0,0)),
                pl.BlockSpec((9,128), lambda i,*_:(0,0)),
            ],
            out_specs=(pl.BlockSpec((3,npts//128,128), lambda i,*_:(0,0,0)), pl.BlockSpec((9,128), lambda i,*_:(0,0))),
            scratch_shapes=[pltpu.VMEM((blocks_n*PH*8,PL),F32), pltpu.VMEM((UN,192,128),F32), pltpu.VMEM((UN,64,128),F32), pltpu.VMEM((UN,64,128),F32)],
        ),
        compiler_params=pltpu.CompilerParams(dimension_semantics=("arbitrary",), vmem_limit_bytes=60*1024*1024),
        name="reduce_points",
    )(tb,tp,word,inc,cj,pj,oc,op,cameras,increment)

CT=10
def project_body(chunk, tb, tp, cam_ref, pts_ref, oc_ref, op_ref, ob_ref, res_ref, cost_ref):
    step=pl.program_id(0)
    groups=chunk//GROUP
    row_id=lax.broadcasted_iota(jnp.int32,(8,128),0)
    @pl.when(step==0)
    def _():
        cost_ref[...]=jnp.zeros_like(cost_ref)
    def one(g):
        base=step*(chunk//TILE)+g*TPG
        cams=[tb[base+i]*CT for i in range(TPG)]
        pts=[tp[base+i]*2 for i in range(TPG)]
        at8=pl.ds(pl.multiple_of(g*8,8),8)
        cam=oc_ref[at8,:]; pid=op_ref[at8,:]
        half=pts_ref.shape[0]//3
        upper=pid>=128; plow=pid&127
        def look(r): return lane_gather(tile_rows([spread(cam_ref,c+r) for c in cams],row_id),cam)
        def lookp(r):
            a=lane_gather(tile_rows([spread(pts_ref,p+r*half) for p in pts],row_id),plow)
            b=lane_gather(tile_rows([spread(pts_ref,p+r*half+1) for p in pts],row_id),plow)
            return jnp.where(upper,b,a)
        x,y,z=lookp(0),lookp(1),lookp(2)
        vx,vy,vz,r,t0,t1,t2,f0,f1,f2=[look(i) for i in range(CT)]
        ax=vy*z-vz*y; ay=vz*x-vx*z; az=vx*y-vy*x
        px=x+r*ax+(vy*az-vz*ay)+t0
        py=y+r*ay+(vz*ax-vx*az)+t1
        pz=z+r*az+(vx*ay-vy*ax)+t2
        inv=1.0/jnp.maximum(-pz,1.0)
        u=px*inv; v=py*inv
        q=u*u+v*v
        fac=f0+q*(f1+q*f2)
        o0=pl.ds(g*16,8,stride=2); o1=pl.ds(g*16+1,8,stride=2)
        ru=fac*u-ob_ref[o0,:]; rv=fac*v-ob_ref[o1,:]
        res_ref[o0,:]=ru; res_ref[o1,:]=rv
        return ru*ru+rv*rv
    def body(i,c):
        for u in range(8): c=c+one(i*8+u)
        return c
    cost_ref[...]+=lax.fori_loop(0,groups//8,body,jnp.zeros((8,128),F32))

def project_points(cam, pts, oc, op, ob, tb, tp, chunk=32768):
    n=oc.shape[0]*128
    return pl.pallas_call(
        functools.partial(project_body, chunk),
        out_shape=(jax.ShapeDtypeStruct((n//64,128),F32), jax.ShapeDtypeStruct((8,128),F32)),
        grid_spec=pltpu.PrefetchScalarGridSpec(
            num_scalar_prefetch=2, grid=(n//chunk,),
            in_specs=[
                pl.BlockSpec(cam.shape, lambda i,*_:(0,0)),
                pl.BlockSpec(pts.shape, lambda i,*_:(0,0)),
                pl.BlockSpec((chunk//128,128), lambda i,*_:(i,0)),
                pl.BlockSpec((chunk//128,128), lambda i,*_:(i,0)),
                pl.BlockSpec((chunk//64,128), lambda i,*_:(i,0)),
            ],
            out_specs=(pl.BlockSpec((chunk//64,128), lambda i,*_:(i,0)), pl.BlockSpec((8,128), lambda i,*_:(0,0))),
        ),
        compiler_params=pltpu.CompilerParams(dimension_semantics=("arbitrary",), vmem_limit_bytes=60*1024*1024),
        name="project_points",
    )(tb,tp,cam,pts,oc,op,ob)


MESH = pl.DeviceIdType.MESH
X, Y, CORE, CAM = "pts_0", "pts_1", "pts_2", "cam"
PTS = (X, Y, CORE)
PTS_CAM = PTS + (CAM,)


def peer(axis, hop):
    n = lax.axis_size(axis)
    return {axis: lax.rem(lax.axis_index(axis) + hop, n)}


def greet(peers):
    barrier = pltpu.get_barrier_semaphore()
    for p in peers:
        pl.semaphore_signal(barrier, inc=1, device_id=p, device_id_type=MESH)
    pl.semaphore_wait(barrier, len(peers))


def hops(axis):
    return range(1, lax.axis_size(axis))


def send(src, dst, send_sem, recv_sem, to):
    copy = pltpu.make_async_remote_copy(src, dst, send_sem, recv_sem, device_id=to, device_id_type=MESH)
    copy.start()
    return copy


def gather_body(local_ref, out_ref, local_sem, send_sem, recv_sem):
    at = {a: lax.axis_index(a) for a in (X, Y, CORE, CAM)}

    def part(k, whole):
        i = [slice(None) if a in whole else at[a] for a in (X, Y, CORE, CAM)]
        return out_ref.at[(*i, pl.ds(3 * k, 3))]

    own = out_ref.at[at[X], at[Y], at[CORE], at[CAM]]
    mine = pltpu.make_async_copy(local_ref, own, local_sem)
    mine.start()
    greet([peer(a, h) for a in (CAM, Y, X, CORE) for h in hops(a)])
    mine.wait()
    order = ((CAM, Y, X), (Y, X, CAM), (X, CAM, Y))
    slot = 0
    for stage in range(3):
        copies = []
        for h in hops(CAM):
            for k in range(3):
                axis, done = order[k][stage], order[k][:stage]
                copies.append(send(part(k, done), part(k, done), send_sem.at[slot], recv_sem.at[slot], peer(axis, h)))
                slot += 1
        for cp in copies:
            cp.wait()
    half = out_ref.at[:, :, at[CORE]]
    send(half, half, send_sem.at[slot], recv_sem.at[slot], peer(CORE, 1)).wait()


def gather_rows(local):
    rows = local.shape[0]
    nx, ny, nc, nz = [lax.axis_size(a) for a in (X, Y, CORE, CAM)]
    out = pl.pallas_call(
        gather_body,
        out_shape=jax.ShapeDtypeStruct((nx, ny, nc, nz, rows, 1, 128), F32),
        in_specs=[pl.BlockSpec(memory_space=pltpu.VMEM)],
        out_specs=pl.BlockSpec(memory_space=pltpu.VMEM),
        scratch_shapes=[pltpu.SemaphoreType.DMA, pltpu.SemaphoreType.DMA((28,)), pltpu.SemaphoreType.DMA((28,))],
        compiler_params=pltpu.CompilerParams(collective_id=0, has_side_effects=True),
        name="gather_rows",
    )(local.reshape(rows, 1, 128))
    return out.reshape(nx * ny * nc * nz * rows, 128)


def cost_peers():
    near = [{**peer(Y, i), **peer(CAM, j)} for i in range(4) for j in range(4) if i or j]
    far = [{**peer(X, i), **peer(CORE, j)} for i in range(4) for j in range(2) if i or j]
    return near, far


def cost_body(scale, part_ref, out_ref, buf, send_sem, recv_sem):
    x, y, c, z = [lax.axis_index(a) for a in (X, Y, CORE, CAM)]
    peers = cost_peers()
    greet(peers[0] + peers[1])
    value = part_ref[...]
    slot = 0
    for stage, (me, count) in enumerate(((y * 4 + z, 16), (x * 2 + c, 8))):
        buf[stage, pl.ds(pl.multiple_of(me * 8, 8), 8), :] = value
        own = buf.at[stage, pl.ds(pl.multiple_of(me * 8, 8), 8)]
        copies = []
        for p in peers[stage]:
            copies.append(send(own, own, send_sem.at[slot], recv_sem.at[slot], p))
            slot += 1
        for cp in copies:
            cp.wait()
        value = buf[stage, 0:8, :]
        for k in range(1, count):
            value = value + buf[stage, k * 8:k * 8 + 8, :]
    out_ref[...] = jnp.sum(value, axis=(0, 1), keepdims=True) * scale


def total_cost(part, scale):
    out = pl.pallas_call(
        functools.partial(cost_body, scale),
        out_shape=jax.ShapeDtypeStruct((1, 1), F32),
        in_specs=[pl.BlockSpec(memory_space=pltpu.VMEM)],
        out_specs=pl.BlockSpec(memory_space=pltpu.VMEM),
        scratch_shapes=[pltpu.VMEM((2, 128, 128), F32), pltpu.SemaphoreType.DMA((22,)), pltpu.SemaphoreType.DMA((22,))],
        compiler_params=pltpu.CompilerParams(collective_id=1, has_side_effects=True),
        name="total_cost",
    )(part)
    return out.reshape(())


RT2 = math.sqrt(2.0)


def camera_rows(trial):
    w = [trial[i:i + 1] for i in range(3)]
    half = 0.5 * jnp.sqrt(w[0] * w[0] + w[1] * w[1] + w[2] * w[2])
    zero = half == 0.0
    ratio = (0.5 * RT2) * jnp.where(zero, 1.0, jnp.sin(half) / jnp.where(zero, 1.0, half))
    f = trial[6:7]
    return [ratio * a for a in w] + [RT2 * jnp.cos(half), trial[3:4], trial[4:5], trial[5:6], f, f * trial[7:8], f * trial[8:9]]


def solve_body(red_ref, cam_ref, inc_ref, pts_hbm, grad_hbm, inv_hbm, new_ref, tab_ref, pts, grad, inv, pscr, gscr, iscr,
               far, near, total, local_sem, send_sem, recv_sem):
    cx, cy, cc = [lax.axis_index(a) for a in (X, Y, CORE)]
    z = lax.axis_index(CAM)
    n = lax.axis_size(CAM)
    rows = red_ref.shape[1] // n
    half = rows // 2
    lanes = pl.ds(pl.multiple_of(z * (rows * 128), 128), rows * 128)
    loads = [pltpu.make_async_copy(src.at[:, lanes], dst, local_sem.at[i])
             for i, (src, dst) in enumerate(((pts_hbm, pts), (grad_hbm, grad), (inv_hbm, inv)))]
    for cp in loads:
        cp.start()
    right, left = peer(CAM, 1), peer(CAM, n - 1)
    for i, row in enumerate(camera_rows(cam_ref[...] + inc_ref[...])):
        tab_ref[cx, cy, cc, z, i] = row
    greet([peer(a, h) for a in (CAM, Y, X, CORE) for h in hops(a)])

    def spread_table(axis, part, slot):
        return [send(part, part, send_sem.at[slot + h - 1], recv_sem.at[slot + h - 1], peer(axis, h)) for h in hops(axis)]

    table = spread_table(CAM, tab_ref.at[cx, cy, cc, z], 10)

    def at(k):
        return lax.rem(z + k, n) * rows

    a = send(red_ref.at[:, pl.ds(at(2), half)], far.at[0], send_sem.at[0], recv_sem.at[0], right)
    b = send(red_ref.at[:, pl.ds(at(2) + half, half)], far.at[1], send_sem.at[1], recv_sem.at[1], left)
    c = send(red_ref.at[:, pl.ds(at(1) + half, half)], near.at[0, :, pl.ds(half, half)], send_sem.at[2], recv_sem.at[2], right)
    d = send(red_ref.at[:, pl.ds(at(n - 1), half)], near.at[1, :, pl.ds(0, half)], send_sem.at[3], recv_sem.at[3], left)
    a.wait_recv()
    total[0] = red_ref[:, pl.ds(at(1), half), :] + far[0]
    e = send(total.at[0], near.at[0, :, pl.ds(0, half)], send_sem.at[4], recv_sem.at[4], right)
    b.wait_recv()
    total[1] = red_ref[:, pl.ds(at(n - 1) + half, half), :] + far[1]
    f = send(total.at[1], near.at[1, :, pl.ds(half, half)], send_sem.at[5], recv_sem.at[5], left)
    for cp in table:
        cp.wait()
    table = spread_table(Y, tab_ref.at[cx, cy, cc], 13)
    for cp in loads:
        cp.wait()
    c.wait_recv()
    d.wait_recv()
    e.wait_recv()
    f.wait_recv()

    def group(g, _):
        r8 = pl.ds(pl.multiple_of(g * 8, 8), 8)
        for j in range(8):
            l = pl.ds(pl.multiple_of(g * 1024 + j * 128, 128), 128)
            pscr[pl.ds(j * 8, 3), :] = pts[:, l]
            gscr[pl.ds(j * 8, 3), :] = grad[:, l]
            iscr[pl.ds(j * 16, 9), :] = inv[:, l]
        own = pl.ds(pl.multiple_of(z * rows + g * 8, 8), 8)
        res = [gscr[pl.ds(k, 8, stride=8), :]
               - (red_ref[k, own, :] + near[0, k, r8, :] + near[1, k, r8, :]) for k in range(3)]
        for i in range(3):
            step = (iscr[pl.ds(3 * i, 8, stride=16), :] * res[0] + iscr[pl.ds(3 * i + 1, 8, stride=16), :] * res[1]
                    + iscr[pl.ds(3 * i + 2, 8, stride=16), :] * res[2])
            new_ref[i, own, :] = pscr[pl.ds(i, 8, stride=8), :] + step
        return 0

    lax.fori_loop(0, rows // 8, group, 0)
    for cp in (a, b, c, d, e, f):
        cp.wait_send()
    for cp in table:
        cp.wait()
    table = spread_table(X, tab_ref.at[cx, :, cc], 16)
    own = new_ref.at[:, pl.ds(z * rows, rows)]
    g = send(own, own, send_sem.at[6], recv_sem.at[6], right)
    h = send(own, own, send_sem.at[7], recv_sem.at[7], left)
    g.wait_recv()
    first = new_ref.at[:, pl.ds(at(n - 1), half)]
    k = send(first, first, send_sem.at[8], recv_sem.at[8], right)
    h.wait_recv()
    second = new_ref.at[:, pl.ds(at(1) + half, half)]
    m = send(second, second, send_sem.at[9], recv_sem.at[9], left)
    for cp in table:
        cp.wait()
    table = spread_table(CORE, tab_ref.at[:, :, cc], 19)
    k.wait_recv()
    m.wait_recv()
    for cp in (g, h, k, m):
        cp.wait_send()
    for cp in table:
        cp.wait()


def solve_points(reduced, cameras, increment, points, gradient, inverse):
    rows = reduced.shape[1] // 4
    nx, ny, nc, nz = [lax.axis_size(a) for a in (X, Y, CORE, CAM)]
    hbm = pl.BlockSpec(memory_space=pl.ANY)
    vmem = pl.BlockSpec(memory_space=pltpu.VMEM)
    new, table = pl.pallas_call(
        solve_body,
        out_shape=(jax.ShapeDtypeStruct(reduced.shape, F32), jax.ShapeDtypeStruct((nx, ny, nc, nz, CT, 1, 128), F32)),
        in_specs=[vmem, vmem, vmem, hbm, hbm, hbm],
        out_specs=(vmem, vmem),
        scratch_shapes=[
            pltpu.VMEM((3, rows * 128), F32), pltpu.VMEM((3, rows * 128), F32), pltpu.VMEM((9, rows * 128), F32),
            pltpu.VMEM((64, 128), F32), pltpu.VMEM((64, 128), F32), pltpu.VMEM((128, 128), F32),
            pltpu.VMEM((2, 3, rows // 2, 128), F32), pltpu.VMEM((2, 3, rows, 128), F32),
            pltpu.VMEM((2, 3, rows // 2, 128), F32),
            pltpu.SemaphoreType.DMA((3,)), pltpu.SemaphoreType.DMA((20,)), pltpu.SemaphoreType.DMA((20,)),
        ],
        compiler_params=pltpu.CompilerParams(collective_id=2, has_side_effects=True, vmem_limit_bytes=60 * 1024 * 1024),
        name="solve_points",
    )(reduced, cameras, increment, points, gradient, inverse)
    return new, table.reshape(nx * ny * nc * nz * CT, 128)


def rows_of(x):
    n = x.shape[1] // 128
    return x.reshape(x.shape[0], n, 128).transpose(1, 0, 2).reshape(n * x.shape[0], 128)


def on_device(cameras, increment, points, gradient, inverse, cj, pj, observed, tb, tp, oc, op, accept):
    oc2 = oc.reshape(-1, 128)
    op2 = op.reshape(-1, 128)
    reduced, kept = reduce_points(gather_rows(increment), cj, pj, oc2, op2, tb, tp, accept.reshape(1), cameras, increment, points.shape[1])
    new, table = solve_points(reduced, cameras, increment, points, gradient, inverse)
    res, cost = project_points(table, new.reshape(-1, 128), oc2, op2, rows_of(observed), tb, tp)
    n = observed.shape[1]
    residual = res.reshape(n // 128, 2, 128).transpose(1, 0, 2).reshape(2, n)
    total = total_cost(cost, 1.0 / (2.0 * n * lax.axis_size(PTS_CAM)))
    accepted = jnp.where((accept & 1) == 1, new.reshape(3, -1), points)
    return residual, total, accepted, kept


def solution(mesh):
    split = Mesh(mesh.devices.reshape(4, 4, 2, mesh.shape["cam"]), PTS_CAM)
    in_specs = (P(None, PTS_CAM), P(None, PTS_CAM), P(None, PTS), P(None, PTS), P(None, PTS),
                P(None, PTS_CAM), P(None, PTS_CAM), P(None, PTS_CAM),
                P(PTS_CAM), P(PTS_CAM), P(PTS_CAM), P(PTS_CAM), P())
    out_specs = (P(None, PTS_CAM), P(), P(None, PTS), P(None, PTS_CAM))
    return jax.shard_map(on_device, mesh=split, in_specs=in_specs, out_specs=out_specs, check_vma=False)
```

time: 310 us -> 107 us (0.35)
  blocking collectives: 191 us -> 0 us
  Pallas kernels: 83.6 us -> 101 us
  between operations: 16.7 us -> 3.09 us
  other arithmetic: 14.7 us -> 1.64 us
    all_gather x2 -> x0, blocking collectives: 125 us -> none  [the longest x1 64.1 us: on_device(): inc_tab = lax.all_gather(increment, PTS_CAM, axis=0, tiled=True)]
    psum x1 -> x0, blocking collectives: 65.2 us -> none  [on_device(): total = lax.psum(jnp.sum(cost), PTS_CAM)]
    pallas_call x0 -> x3, Pallas kernels: none -> 59.3 us  [the longest x1 22.3 us: solve_points(): pl.pallas_call(solve_body, out_shape=(jax.ShapeDtypeStruct(reduced.shape,...]
    pallas_call x1, Pallas kernels: 63.5 us -> 28.9 us  [reduce_points(): pl.pallas_call(functools.partial(reduce_body, chunk, blocks_n), out_shape...]
    add x3 -> x0, other arithmetic: 12.5 us -> none  [the longest x1 9.97 us: on_device(): inverse[3 * i] * d[0] + inverse[3 * i + 1] * d[1]]
    pallas_call x1, Pallas kernels: 20.1 us -> 12.6 us  [project_points(): pl.pallas_call(functools.partial(project_body, chunk), out_shape=(jax.Sha...]
    unnamed x28 -> x4, local copies, waits for them, and re-layouts: 4 us -> 0.01 us
  transfers between devices with their start and end apart: 1 -> 0, of which waited for: 0 -> 0; matrix products, arithmetic and copies ran while one was open for 0% -> 0% of each run, Pallas kernels for 0% -> 0%
where the time goes in v2:
time: 107 us
  Pallas kernels  101 us (94%)
  between operations  3.09 us (3%)
  other arithmetic  1.64 us (2%)
  local copies, waits for them, and re-layouts  1.31 us (1%)
    pallas_call x1, Pallas kernels, reduce_points(): pl.pallas_call(functools.partial(reduce_body, chunk, blocks_n), out_shape...  28.9 us
    pallas_call x1, Pallas kernels, solve_points(): pl.pallas_call(solve_body, out_shape=(jax.ShapeDtypeStruct(reduced.shape,...  22.3 us
    pallas_call x1, Pallas kernels, gather_rows(): pl.pallas_call(gather_body, out_shape=jax.ShapeDtypeStruct((nx, ny, nc, n...  21.7 us
    pallas_call x1, Pallas kernels, total_cost(): pl.pallas_call(functools.partial(cost_body, scale), out_shape=jax.ShapeDt...  15.4 us
    pallas_call x1, Pallas kernels, project_points(): pl.pallas_call(functools.partial(project_body, chunk), out_shape=(jax.Sha...  12.6 us

profile of v2, /device:TPU:1, one launch (start us, length us, event | category | flops | bytes accessed | tf_op | source)
XLA Modules:
  0.0 106.9 jit_solution(566120475404695252)
XLA Ops:
  1.3 1.3 %reshape.48.local_ref = f32[9,1,128]{2,1,0:T(1,128)} reshape(f32[9,128]{1,0:T(8,128)} %inc_ref.1) | data formatting | bytes 9216 | tf_op jit(solution)/shard_map/reshape | solution.py:247
  2.6 21.7 %gather_rows.1 = f32[4,4,2,4,9,1,128]{6,5,4,3,2,1,0:T(1,128)} custom-call(f32[9,1,128]{2,1,0:T(1,128)} %reshape.48.local_ref), custom_call_target="tpu_custom_call" | custom-call | tf_op jit(solution)/shard_map/gather_rows/pallas_call | solution.py:239
  24.2 28.9 %reduce_points.1 = (f32[3,512,128]{2,1,0:T(8,128)}, f32[9,128]{1,0:T(8,128)}) custom-call(s32[1024]{0:T(1024)} %tb.3, s32[1024]{0:T(1024)} %tp.3, s32[1]{0:T(128)} %bitcast.20.word, f32[1152,128]{1,0:T(8,128)} %bitcast.27, bf16[18,262144]{1,0:T(8,128)(2,1)} %cj_ref.1, bf16[6,262144]{1,0:T(8,128)(2,1)} %pj_ref.1, s32[2048,128]{1,0:T(8,128)} %bitcast.21, ...), custom_call_target="tpu_custom_call" | custom-call | tf_op jit(solution)/shard_map/reduce_points/pallas_call | solution.py:99
  53.2 22.3 %solve_points.1 = (f32[3,512,128]{2,1,0:T(8,128)}, f32[4,4,2,4,10,1,128]{6,5,4,3,2,1,0:T(1,128)}) custom-call(f32[3,512,128]{2,1,0:T(8,128)} %get-tuple-element.10.red_ref, f32[9,128]{1,0:T(8,128)} %cam_ref.3, f32[9,128]{1,0:T(8,128)} %inc_ref.1, f32[3,65536]{1,0:T(4,128)} %pts_hbm.1, f32[3,65536]{1,0:T(4,128)} %grad_hbm.1, f32[9,65536]{1,0:T(8,128)} %inv_hbm.1), custom_call_target="tpu_custom_call" | custom-call | tf_op jit(solution)/shard_map/solve_points/pallas_call | solution.py:395
  75.5 0.0 copy-start
  75.5 0.0 copy-start.1
  75.5 12.6 %project_points.1 = (f32[4096,128]{1,0:T(8,128)}, f32[8,128]{1,0:T(8,128)}) custom-call(s32[1024]{0:T(1024)} %tb.3, s32[1024]{0:T(1024)} %tp.3, f32[1280,128]{1,0:T(8,128)} %bitcast.29, f32[1536,128]{1,0:T(8,128)} %bitcast.25, s32[2048,128]{1,0:T(8,128)} %bitcast.22, s32[2048,128]{1,0:T(8,128)} %bitcast.24, f32[4096,128]{1,0:T(8,128)} %bitcast.28), custom_call_target="tpu_custom_call" | custom-call | tf_op jit(solution)/shard_map/project_points/pallas_call | solution.py:162
  88.1 15.4 %total_cost.1 = f32[1,1]{1,0:T(1,128)} custom-call(f32[8,128]{1,0:T(8,128)} %get-tuple-element.14.part_ref), custom_call_target="tpu_custom_call" | custom-call | tf_op jit(solution)/shard_map/total_cost/pallas_call | solution.py:279
  103.5 0.0 copy-done
  103.5 0.0 copy-done.1
  103.5 1.6 %bitcast_select_fusion = f32[3,65536]{1,0:T(4,128)} fusion(f32[3,65536]{1,0:T(4,128)S(1)} %copy-done, f32[1,3,512,128]{3,2,1,0:T(8,128)S(1)} %bitcast.26, pred[]{:T(512)S(6)} %eq.3), kind=kLoop, calls=%fused_computation | loop fusion | flops 196608 | bytes 2359297 | tf_op jit(solution)/shard_map/jit(_where)/select_n | solution.py:427
Async XLA Ops:
  75.5 28.0 %copy-start = (f32[3,65536]{1,0:T(4,128)S(1)}, f32[3,65536]{1,0:T(4,128)}, u32[]{:S(2)}) copy-start(f32[3,65536]{1,0:T(4,128)} %pts_hbm.1) | copy-start | bytes 2359300
  75.5 28.0 %copy-start.1 = (f32[3,512,128]{2,1,0:T(8,128)S(1)}, f32[3,512,128]{2,1,0:T(8,128)}, u32[]{:S(2)}) copy-start(f32[3,512,128]{2,1,0:T(8,128)} %get-tuple-element.12) | copy-start | bytes 2359300

commit v3 on v2

--- a/solution.py
+++ b/solution.py
@@ -93,7 +93,7 @@
             return 0
         lax.fori_loop(0, blocks_n, flush, 0, unroll=8)
 
-def reduce_points(inc, cj, pj, oc, op, tb, tp, word, cameras, increment, npts, chunk=32768):
+def reduce_points(inc, cj, pj, oc, op, tb, tp, word, cameras, increment, npts, chunk=16384):
     n=cj.shape[1]
     blocks_n=npts//PB
     return pl.pallas_call(
@@ -206,18 +206,16 @@
     return copy
 
 
-def gather_body(local_ref, out_ref, local_sem, send_sem, recv_sem):
+def gather_body(local_ref, out_ref, send_sem, recv_sem):
     at = {a: lax.axis_index(a) for a in (X, Y, CORE, CAM)}
 
     def part(k, whole):
         i = [slice(None) if a in whole else at[a] for a in (X, Y, CORE, CAM)]
         return out_ref.at[(*i, pl.ds(3 * k, 3))]
 
-    own = out_ref.at[at[X], at[Y], at[CORE], at[CAM]]
-    mine = pltpu.make_async_copy(local_ref, own, local_sem)
-    mine.start()
+    for i in range(9):
+        out_ref[at[X], at[Y], at[CORE], at[CAM], i] = local_ref[i:i + 1, :]
     greet([peer(a, h) for a in (CAM, Y, X, CORE) for h in hops(a)])
-    mine.wait()
     order = ((CAM, Y, X), (Y, X, CAM), (X, CAM, Y))
     slot = 0
     for stage in range(3):
@@ -241,10 +239,10 @@
         out_shape=jax.ShapeDtypeStruct((nx, ny, nc, nz, rows, 1, 128), F32),
         in_specs=[pl.BlockSpec(memory_space=pltpu.VMEM)],
         out_specs=pl.BlockSpec(memory_space=pltpu.VMEM),
-        scratch_shapes=[pltpu.SemaphoreType.DMA, pltpu.SemaphoreType.DMA((28,)), pltpu.SemaphoreType.DMA((28,))],
+        scratch_shapes=[pltpu.SemaphoreType.DMA((28,)), pltpu.SemaphoreType.DMA((28,))],
         compiler_params=pltpu.CompilerParams(collective_id=0, has_side_effects=True),
         name="gather_rows",
-    )(local.reshape(rows, 1, 128))
+    )(local)
     return out.reshape(nx * ny * nc * nz * rows, 128)
 
 
@@ -361,27 +359,30 @@
             new_ref[i, own, :] = pscr[pl.ds(i, 8, stride=8), :] + step
         return 0
 
-    lax.fori_loop(0, rows // 8, group, 0)
-    for cp in (a, b, c, d, e, f):
-        cp.wait_send()
+    def own(part):
+        return new_ref.at[:, pl.ds(z * rows + part * half, half)]
+
+    lax.fori_loop(0, half // 8, group, 0)
+    g = send(own(0), own(0), send_sem.at[6], recv_sem.at[6], right)
+    lax.fori_loop(half // 8, rows // 8, group, 0)
+    h = send(own(1), own(1), send_sem.at[7], recv_sem.at[7], left)
+    g2 = send(own(1), own(1), send_sem.at[8], recv_sem.at[8], right)
+    h2 = send(own(0), own(0), send_sem.at[9], recv_sem.at[9], left)
     for cp in table:
         cp.wait()
     table = spread_table(X, tab_ref.at[cx, :, cc], 16)
-    own = new_ref.at[:, pl.ds(z * rows, rows)]
-    g = send(own, own, send_sem.at[6], recv_sem.at[6], right)
-    h = send(own, own, send_sem.at[7], recv_sem.at[7], left)
     g.wait_recv()
     first = new_ref.at[:, pl.ds(at(n - 1), half)]
-    k = send(first, first, send_sem.at[8], recv_sem.at[8], right)
+    k = send(first, first, send_sem.at[20], recv_sem.at[20], right)
     h.wait_recv()
     second = new_ref.at[:, pl.ds(at(1) + half, half)]
-    m = send(second, second, send_sem.at[9], recv_sem.at[9], left)
+    m = send(second, second, send_sem.at[21], recv_sem.at[21], left)
     for cp in table:
         cp.wait()
     table = spread_table(CORE, tab_ref.at[:, :, cc], 19)
-    k.wait_recv()
-    m.wait_recv()
-    for cp in (g, h, k, m):
+    for cp in (g2, h2, k, m):
+        cp.wait_recv()
+    for cp in (a, b, c, d, e, f, g, h, g2, h2, k, m):
         cp.wait_send()
     for cp in table:
         cp.wait()
@@ -402,7 +403,7 @@
             pltpu.VMEM((64, 128), F32), pltpu.VMEM((64, 128), F32), pltpu.VMEM((128, 128), F32),
             pltpu.VMEM((2, 3, rows // 2, 128), F32), pltpu.VMEM((2, 3, rows, 128), F32),
             pltpu.VMEM((2, 3, rows // 2, 128), F32),
-            pltpu.SemaphoreType.DMA((3,)), pltpu.SemaphoreType.DMA((20,)), pltpu.SemaphoreType.DMA((20,)),
+            pltpu.SemaphoreType.DMA((3,)), pltpu.SemaphoreType.DMA((22,)), pltpu.SemaphoreType.DMA((22,)),
         ],
         compiler_params=pltpu.CompilerParams(collective_id=2, has_side_effects=True, vmem_limit_bytes=60 * 1024 * 1024),
         name="solve_points",

time: 107 us -> 105 us (0.981)
  local copies, waits for them, and re-layouts: 1.31 us -> 0.01 us
  Pallas kernels: 101 us -> 99.9 us
    reshape x1 -> x0, local copies, waits for them, and re-layouts: 1.29 us -> none  [gather_rows(): local.reshape(rows, 1, 128)]
where the time goes in v3:
time: 105 us
  Pallas kernels  99.9 us (95%)
  between operations  3.09 us (3%)
  other arithmetic  1.64 us (2%)
    pallas_call x1, Pallas kernels, reduce_points(): pl.pallas_call(functools.partial(reduce_body, chunk, blocks_n), out_shape...  28.8 us
    pallas_call x1, Pallas kernels, gather_rows(): pl.pallas_call(gather_body, out_shape=jax.ShapeDtypeStruct((nx, ny, nc, n...  21.7 us
    pallas_call x1, Pallas kernels, solve_points(): pl.pallas_call(solve_body, out_shape=(jax.ShapeDtypeStruct(reduced.shape,...  21.7 us
    pallas_call x1, Pallas kernels, total_cost(): pl.pallas_call(functools.partial(cost_body, scale), out_shape=jax.ShapeDt...  15.1 us
    pallas_call x1, Pallas kernels, project_points(): pl.pallas_call(functools.partial(project_body, chunk), out_shape=(jax.Sha...  12.6 us

profile of v3, /device:TPU:1, one launch (start us, length us, event | category | flops | bytes accessed | tf_op | source)
XLA Modules:
  0.0 104.7 jit_solution(3504099611120008151)
XLA Ops:
  1.3 21.7 %gather_rows.1 = f32[4,4,2,4,9,1,128]{6,5,4,3,2,1,0:T(1,128)} custom-call(f32[9,128]{1,0:T(8,128)} %inc_ref.1), custom_call_target="tpu_custom_call" | custom-call | tf_op jit(solution)/shard_map/gather_rows/pallas_call | solution.py:237
  23.0 28.8 %reduce_points.1 = (f32[3,512,128]{2,1,0:T(8,128)}, f32[9,128]{1,0:T(8,128)}) custom-call(s32[1024]{0:T(1024)} %tb.3, s32[1024]{0:T(1024)} %tp.3, s32[1]{0:T(128)} %bitcast.20.word, f32[1152,128]{1,0:T(8,128)} %bitcast.27, bf16[18,262144]{1,0:T(8,128)(2,1)} %cj_ref.1, bf16[6,262144]{1,0:T(8,128)(2,1)} %pj_ref.1, s32[2048,128]{1,0:T(8,128)} %bitcast.21, ...), custom_call_target="tpu_custom_call" | custom-call | tf_op jit(solution)/shard_map/reduce_points/pallas_call | solution.py:99
  51.8 21.7 %solve_points.1 = (f32[3,512,128]{2,1,0:T(8,128)}, f32[4,4,2,4,10,1,128]{6,5,4,3,2,1,0:T(1,128)}) custom-call(f32[3,512,128]{2,1,0:T(8,128)} %get-tuple-element.10.red_ref, f32[9,128]{1,0:T(8,128)} %cam_ref.3, f32[9,128]{1,0:T(8,128)} %inc_ref.1, f32[3,65536]{1,0:T(4,128)} %pts_hbm.1, f32[3,65536]{1,0:T(4,128)} %grad_hbm.1, f32[9,65536]{1,0:T(8,128)} %inv_hbm.1), custom_call_target="tpu_custom_call" | custom-call | tf_op jit(solution)/shard_map/solve_points/pallas_call | solution.py:396
  73.5 0.0 copy-start
  73.5 0.0 copy-start.1
  73.6 12.6 %project_points.1 = (f32[4096,128]{1,0:T(8,128)}, f32[8,128]{1,0:T(8,128)}) custom-call(s32[1024]{0:T(1024)} %tb.3, s32[1024]{0:T(1024)} %tp.3, f32[1280,128]{1,0:T(8,128)} %bitcast.29, f32[1536,128]{1,0:T(8,128)} %bitcast.25, s32[2048,128]{1,0:T(8,128)} %bitcast.22, s32[2048,128]{1,0:T(8,128)} %bitcast.24, f32[4096,128]{1,0:T(8,128)} %bitcast.28), custom_call_target="tpu_custom_call" | custom-call | tf_op jit(solution)/shard_map/project_points/pallas_call | solution.py:162
  86.1 15.1 %total_cost.1 = f32[1,1]{1,0:T(1,128)} custom-call(f32[8,128]{1,0:T(8,128)} %get-tuple-element.14.part_ref), custom_call_target="tpu_custom_call" | custom-call | tf_op jit(solution)/shard_map/total_cost/pallas_call | solution.py:277
  101.2 0.0 copy-done
  101.3 0.0 copy-done.1
  101.3 1.6 %bitcast_select_fusion = f32[3,65536]{1,0:T(4,128)} fusion(f32[3,65536]{1,0:T(4,128)S(1)} %copy-done, f32[1,3,512,128]{3,2,1,0:T(8,128)S(1)} %bitcast.26, pred[]{:T(512)S(6)} %eq.3), kind=kLoop, calls=%fused_computation | loop fusion | flops 196608 | bytes 2359297 | tf_op jit(solution)/shard_map/jit(_where)/select_n | solution.py:428
Async XLA Ops:
  73.5 27.7 %copy-start = (f32[3,65536]{1,0:T(4,128)S(1)}, f32[3,65536]{1,0:T(4,128)}, u32[]{:S(2)}) copy-start(f32[3,65536]{1,0:T(4,128)} %pts_hbm.1) | copy-start | bytes 2359300
  73.5 27.7 %copy-start.1 = (f32[3,512,128]{2,1,0:T(8,128)S(1)}, f32[3,512,128]{2,1,0:T(8,128)}, u32[]{:S(2)}) copy-start(f32[3,512,128]{2,1,0:T(8,128)} %get-tuple-element.12) | copy-start | bytes 2359300

commit v4 on v3

--- a/solution.py
+++ b/solution.py
@@ -25,7 +25,7 @@
     return ref[pl.ds(first, 8, stride=0), :]
 
 PH=8; PL=32
-UN=8
+UN=16
 
 def reduce_body(chunk, blocks_n, tb, tp, word, inc_ref, cj_ref, pj_ref, oc_ref, op_ref, cam_ref, own_ref, out_ref, kept_ref, acc, jscr, pscr, wscr):
     step = pl.program_id(0)
@@ -91,7 +91,7 @@
                 for n in range(3):
                     out_ref[n, pl.ds(2*i+h,1),:] = s[n:n+1,:]
             return 0
-        lax.fori_loop(0, blocks_n, flush, 0, unroll=8)
+        lax.fori_loop(0, blocks_n, flush, 0, unroll=32)
 
 def reduce_points(inc, cj, pj, oc, op, tb, tp, word, cameras, increment, npts, chunk=16384):
     n=cj.shape[1]
@@ -153,11 +153,11 @@
         res_ref[o0,:]=ru; res_ref[o1,:]=rv
         return ru*ru+rv*rv
     def body(i,c):
-        for u in range(8): c=c+one(i*8+u)
+        for u in range(16): c=c+one(i*16+u)
         return c
-    cost_ref[...]+=lax.fori_loop(0,groups//8,body,jnp.zeros((8,128),F32))
-
-def project_points(cam, pts, oc, op, ob, tb, tp, chunk=32768):
+    cost_ref[...]+=lax.fori_loop(0,groups//16,body,jnp.zeros((8,128),F32))
+
+def project_points(cam, pts, oc, op, ob, tb, tp, chunk=65536):
     n=oc.shape[0]*128
     return pl.pallas_call(
         functools.partial(project_body, chunk),
@@ -217,18 +217,26 @@
         out_ref[at[X], at[Y], at[CORE], at[CAM], i] = local_ref[i:i + 1, :]
     greet([peer(a, h) for a in (CAM, Y, X, CORE) for h in hops(a)])
     order = ((CAM, Y, X), (Y, X, CAM), (X, CAM, Y))
-    slot = 0
-    for stage in range(3):
-        copies = []
-        for h in hops(CAM):
-            for k in range(3):
-                axis, done = order[k][stage], order[k][:stage]
-                copies.append(send(part(k, done), part(k, done), send_sem.at[slot], recv_sem.at[slot], peer(axis, h)))
-                slot += 1
-        for cp in copies:
-            cp.wait()
+    def start(k, stage):
+        axis, done = order[k][stage], order[k][:stage]
+        first = 9 * k + 3 * stage
+        return [send(part(k, done), part(k, done), send_sem.at[first + h - 1], recv_sem.at[first + h - 1], peer(axis, h))
+                for h in hops(axis)]
+
+    sent = []
+    flying = [start(k, 0) for k in range(3)]
+    for stage in range(1, 4):
+        for k in range(3):
+            for cp in flying[k]:
+                cp.wait_recv()
+            sent += flying[k]
+            if stage < 3:
+                flying[k] = start(k, stage)
     half = out_ref.at[:, :, at[CORE]]
-    send(half, half, send_sem.at[slot], recv_sem.at[slot], peer(CORE, 1)).wait()
+    last = send(half, half, send_sem.at[27], recv_sem.at[27], peer(CORE, 1))
+    for cp in sent:
+        cp.wait_send()
+    last.wait()
 
 
 def gather_rows(local):

time: 105 us -> 101 us (0.962)
  Pallas kernels: 99.9 us -> 95.1 us
    pallas_call x1, Pallas kernels: 28.8 us -> 25.2 us  [reduce_points(): pl.pallas_call(functools.partial(reduce_body, chunk, blocks_n), out_shape...]
    pallas_call x1, Pallas kernels: 12.6 us -> 11.3 us  [project_points(): pl.pallas_call(functools.partial(project_body, chunk), out_shape=(jax.Sha...]
where the time goes in v4:
time: 101 us; the launch traced here: 99.9 us
  Pallas kernels  95.1 us (94%)
  between operations  3.09 us (3%)
  other arithmetic  1.64 us (2%)
    pallas_call x1, Pallas kernels, reduce_points(): pl.pallas_call(functools.partial(reduce_body, chunk, blocks_n), out_shape...  25.2 us
    pallas_call x1, Pallas kernels, solve_points(): pl.pallas_call(solve_body, out_shape=(jax.ShapeDtypeStruct(reduced.shape,...  21.9 us
    pallas_call x1, Pallas kernels, gather_rows(): pl.pallas_call(gather_body, out_shape=jax.ShapeDtypeStruct((nx, ny, nc, n...  21.7 us
    pallas_call x1, Pallas kernels, total_cost(): pl.pallas_call(functools.partial(cost_body, scale), out_shape=jax.ShapeDt...  15.1 us
    pallas_call x1, Pallas kernels, project_points(): pl.pallas_call(functools.partial(project_body, chunk), out_shape=(jax.Sha...  11.3 us

profile of v4, /device:TPU:1, one launch (start us, length us, event | category | flops | bytes accessed | tf_op | source)
XLA Modules:
  0.0 99.9 jit_solution(12059887326931269019)
XLA Ops:
  1.3 21.7 %gather_rows.1 = f32[4,4,2,4,9,1,128]{6,5,4,3,2,1,0:T(1,128)} custom-call(f32[9,128]{1,0:T(8,128)} %inc_ref.1), custom_call_target="tpu_custom_call" | custom-call | tf_op jit(solution)/shard_map/gather_rows/pallas_call | solution.py:245
  23.0 25.2 %reduce_points.1 = (f32[3,512,128]{2,1,0:T(8,128)}, f32[9,128]{1,0:T(8,128)}) custom-call(s32[1024]{0:T(1024)} %tb.3, s32[1024]{0:T(1024)} %tp.3, s32[1]{0:T(128)} %bitcast.20.word, f32[1152,128]{1,0:T(8,128)} %bitcast.27, bf16[18,262144]{1,0:T(8,128)(2,1)} %cj_ref.1, bf16[6,262144]{1,0:T(8,128)(2,1)} %pj_ref.1, s32[2048,128]{1,0:T(8,128)} %bitcast.21, ...), custom_call_target="tpu_custom_call" | custom-call | tf_op jit(solution)/shard_map/reduce_points/pallas_call | solution.py:99
  48.2 21.9 %solve_points.1 = (f32[3,512,128]{2,1,0:T(8,128)}, f32[4,4,2,4,10,1,128]{6,5,4,3,2,1,0:T(1,128)}) custom-call(f32[3,512,128]{2,1,0:T(8,128)} %get-tuple-element.10.red_ref, f32[9,128]{1,0:T(8,128)} %cam_ref.3, f32[9,128]{1,0:T(8,128)} %inc_ref.1, f32[3,65536]{1,0:T(4,128)} %pts_hbm.1, f32[3,65536]{1,0:T(4,128)} %grad_hbm.1, f32[9,65536]{1,0:T(8,128)} %inv_hbm.1), custom_call_target="tpu_custom_call" | custom-call | tf_op jit(solution)/shard_map/solve_points/pallas_call | solution.py:404
  70.1 0.0 copy-start
  70.1 0.0 copy-start.1
  70.1 11.3 %project_points.1 = (f32[4096,128]{1,0:T(8,128)}, f32[8,128]{1,0:T(8,128)}) custom-call(s32[1024]{0:T(1024)} %tb.3, s32[1024]{0:T(1024)} %tp.3, f32[1280,128]{1,0:T(8,128)} %bitcast.29, f32[1536,128]{1,0:T(8,128)} %bitcast.25, s32[2048,128]{1,0:T(8,128)} %bitcast.22, s32[2048,128]{1,0:T(8,128)} %bitcast.24, f32[4096,128]{1,0:T(8,128)} %bitcast.28), custom_call_target="tpu_custom_call" | custom-call | tf_op jit(solution)/shard_map/project_points/pallas_call | solution.py:162
  81.4 15.1 %total_cost.1 = f32[1,1]{1,0:T(1,128)} custom-call(f32[8,128]{1,0:T(8,128)} %get-tuple-element.14.part_ref), custom_call_target="tpu_custom_call" | custom-call | tf_op jit(solution)/shard_map/total_cost/pallas_call | solution.py:285
  96.5 0.0 copy-done
  96.5 0.0 copy-done.1
  96.5 1.6 %bitcast_select_fusion = f32[3,65536]{1,0:T(4,128)} fusion(f32[3,65536]{1,0:T(4,128)S(1)} %copy-done, f32[1,3,512,128]{3,2,1,0:T(8,128)S(1)} %bitcast.26, pred[]{:T(512)S(6)} %eq.3), kind=kLoop, calls=%fused_computation | loop fusion | flops 196608 | bytes 2359297 | tf_op jit(solution)/shard_map/jit(_where)/select_n | solution.py:436
Async XLA Ops:
  70.1 26.4 %copy-start = (f32[3,65536]{1,0:T(4,128)S(1)}, f32[3,65536]{1,0:T(4,128)}, u32[]{:S(2)}) copy-start(f32[3,65536]{1,0:T(4,128)} %pts_hbm.1) | copy-start | bytes 2359300
  70.1 26.4 %copy-start.1 = (f32[3,512,128]{2,1,0:T(8,128)S(1)}, f32[3,512,128]{2,1,0:T(8,128)}, u32[]{:S(2)}) copy-start(f32[3,512,128]{2,1,0:T(8,128)} %get-tuple-element.12) | copy-start | bytes 2359300

commit v5 on v4

--- a/solution.py
+++ b/solution.py
@@ -113,7 +113,8 @@
             out_specs=(pl.BlockSpec((3,npts//128,128), lambda i,*_:(0,0,0)), pl.BlockSpec((9,128), lambda i,*_:(0,0))),
             scratch_shapes=[pltpu.VMEM((blocks_n*PH*8,PL),F32), pltpu.VMEM((UN,192,128),F32), pltpu.VMEM((UN,64,128),F32), pltpu.VMEM((UN,64,128),F32)],
         ),
-        compiler_params=pltpu.CompilerParams(dimension_semantics=("arbitrary",), vmem_limit_bytes=60*1024*1024),
+        cost_estimate=pl.CostEstimate(flops=10000000000, bytes_accessed=1000000, transcendentals=0),
+        compiler_params=pltpu.CompilerParams(dimension_semantics=("arbitrary",), vmem_limit_bytes=28*1024*1024),
         name="reduce_points",
     )(tb,tp,word,inc,cj,pj,oc,op,cameras,increment)
 
@@ -173,7 +174,8 @@
             ],
             out_specs=(pl.BlockSpec((chunk//64,128), lambda i,*_:(i,0)), pl.BlockSpec((8,128), lambda i,*_:(0,0))),
         ),
-        compiler_params=pltpu.CompilerParams(dimension_semantics=("arbitrary",), vmem_limit_bytes=60*1024*1024),
+        cost_estimate=pl.CostEstimate(flops=5000000000, bytes_accessed=1000000, transcendentals=0),
+        compiler_params=pltpu.CompilerParams(dimension_semantics=("arbitrary",), vmem_limit_bytes=20*1024*1024),
         name="project_points",
     )(tb,tp,cam,pts,oc,op,ob)
 
@@ -248,7 +250,8 @@
         in_specs=[pl.BlockSpec(memory_space=pltpu.VMEM)],
         out_specs=pl.BlockSpec(memory_space=pltpu.VMEM),
         scratch_shapes=[pltpu.SemaphoreType.DMA((28,)), pltpu.SemaphoreType.DMA((28,))],
-        compiler_params=pltpu.CompilerParams(collective_id=0, has_side_effects=True),
+        cost_estimate=pl.CostEstimate(flops=20000000000, bytes_accessed=1000000, transcendentals=0),
+        compiler_params=pltpu.CompilerParams(collective_id=0, has_side_effects=True, vmem_limit_bytes=8*1024*1024),
         name="gather_rows",
     )(local)
     return out.reshape(nx * ny * nc * nz * rows, 128)
@@ -288,7 +291,8 @@
         in_specs=[pl.BlockSpec(memory_space=pltpu.VMEM)],
         out_specs=pl.BlockSpec(memory_space=pltpu.VMEM),
         scratch_shapes=[pltpu.VMEM((2, 128, 128), F32), pltpu.SemaphoreType.DMA((22,)), pltpu.SemaphoreType.DMA((22,))],
-        compiler_params=pltpu.CompilerParams(collective_id=1, has_side_effects=True),
+        cost_estimate=pl.CostEstimate(flops=5000000000, bytes_accessed=1000000, transcendentals=0),
+        compiler_params=pltpu.CompilerParams(collective_id=1, has_side_effects=True, vmem_limit_bytes=4*1024*1024),
         name="total_cost",
     )(part)
     return out.reshape(())
@@ -413,7 +417,8 @@
             pltpu.VMEM((2, 3, rows // 2, 128), F32),
             pltpu.SemaphoreType.DMA((3,)), pltpu.SemaphoreType.DMA((22,)), pltpu.SemaphoreType.DMA((22,)),
         ],
-        compiler_params=pltpu.CompilerParams(collective_id=2, has_side_effects=True, vmem_limit_bytes=60 * 1024 * 1024),
+        cost_estimate=pl.CostEstimate(flops=8000000000, bytes_accessed=1000000, transcendentals=0),
+        compiler_params=pltpu.CompilerParams(collective_id=2, has_side_effects=True, vmem_limit_bytes=16*1024*1024),
         name="solve_points",
     )(reduced, cameras, increment, points, gradient, inverse)
     return new, table.reshape(nx * ny * nc * nz * CT, 128)

time: 101 us -> 93.2 us (0.923)
  Pallas kernels: 95.1 us -> 87.4 us
    pallas_call x1, Pallas kernels: 11.3 us -> 9.17 us  [project_points(): pl.pallas_call(functools.partial(project_body, chunk), out_shape=(jax.Sha...]
    pallas_call x1, Pallas kernels: 21.9 us -> 19.8 us  [solve_points(): pl.pallas_call(solve_body, out_shape=(jax.ShapeDtypeStruct(reduced.shape,...]
    pallas_call x1, Pallas kernels: 21.7 us -> 20.3 us  [gather_rows(): pl.pallas_call(gather_body, out_shape=jax.ShapeDtypeStruct((nx, ny, nc, n...]
    pallas_call x1, Pallas kernels: 25.2 us -> 23.8 us  [reduce_points(): pl.pallas_call(functools.partial(reduce_body, chunk, blocks_n), out_shape...]
where the time goes in v5:
time: 93.2 us; the launch traced here: 93 us
  Pallas kernels  87.4 us (94%)
  between operations  3.21 us (3%)
  other arithmetic  1.64 us (2%)
    pallas_call x1, Pallas kernels, reduce_points(): pl.pallas_call(functools.partial(reduce_body, chunk, blocks_n), out_shape...  23.8 us
    pallas_call x1, Pallas kernels, gather_rows(): pl.pallas_call(gather_body, out_shape=jax.ShapeDtypeStruct((nx, ny, nc, n...  20.3 us
    pallas_call x1, Pallas kernels, solve_points(): pl.pallas_call(solve_body, out_shape=(jax.ShapeDtypeStruct(reduced.shape,...  19.8 us
    pallas_call x1, Pallas kernels, total_cost(): pl.pallas_call(functools.partial(cost_body, scale), out_shape=jax.ShapeDt...  14.4 us
    pallas_call x1, Pallas kernels, project_points(): pl.pallas_call(functools.partial(project_body, chunk), out_shape=(jax.Sha...  9.17 us

profile of v5, /device:TPU:1, one launch (start us, length us, event | category | flops | bytes accessed | tf_op | source)
XLA Modules:
  0.0 93.0 jit_solution(4393374497528923246)
XLA Ops:
  1.3 0.0 copy-start.8
  1.3 0.7 copy-done.8
  2.0 0.0 copy-start.1
  2.0 0.0 copy-start.2
  2.0 0.0 copy-start.6
  2.0 0.0 copy-start.7
  2.0 0.0 copy-start.9
  2.0 0.0 copy-start.10
  2.0 0.0 copy-start.11
  2.0 0.0 copy-start.12
  2.0 20.3 %gather_rows.1 = f32[4,4,2,4,9,1,128]{6,5,4,3,2,1,0:T(1,128)S(1)} custom-call(f32[9,128]{1,0:T(8,128)S(1)} %copy-done.8), custom_call_target="tpu_custom_call" | custom-call | flops 20000000000 | bytes 1000000 | tf_op jit(solution)/shard_map/gather_rows/pallas_call | solution.py:247
  22.3 0.0 copy-done.1
  22.3 0.0 copy-done.2
  22.3 0.0 copy-done.6
  22.3 0.0 copy-done.7
  22.3 0.0 copy-done.9
  22.4 0.0 copy-done.10
  22.4 0.0 copy-done.11
  22.4 0.0 copy-done.12
  22.4 0.0 copy-start
  22.4 0.0 copy-start.3
  22.4 0.0 copy-start.5
  22.4 23.8 %reduce_points.1 = (f32[3,512,128]{2,1,0:T(8,128)S(1)}, f32[9,128]{1,0:T(8,128)}) custom-call(s32[1024]{0:T(1024)S(1)} %copy-done.11, s32[1024]{0:T(1024)S(1)} %copy-done.12, s32[1]{0:T(128)} %bitcast.20.word, f32[1152,128]{1,0:T(8,128)S(1)} %bitcast.29, bf16[18,262144]{1,0:T(8,128)(2,1)S(1)} %copy-done.1, bf16[6,262144]{1,0:T(8,128)(2,1)S(1)} %copy-done.2, ...), custom_call_target="tpu_custom_call" | custom-call | flops 10000000000 | bytes 1000000 | tf_op jit(solution)/shard_map/reduce_points/pallas_call | solution.py:99
  46.2 0.0 copy-done
  46.2 0.0 copy-done.3
  46.2 0.0 copy-done.5
  46.2 0.0 copy-start.4
  46.2 19.8 %solve_points.1 = (f32[3,512,128]{2,1,0:T(8,128)S(1)}, f32[4,4,2,4,10,1,128]{6,5,4,3,2,1,0:T(1,128)S(1)}) custom-call(f32[3,512,128]{2,1,0:T(8,128)S(1)} %get-tuple-element.10.red_ref, f32[9,128]{1,0:T(8,128)S(1)} %copy-done.10, f32[9,128]{1,0:T(8,128)S(1)} %copy-done.9, f32[3,65536]{1,0:T(4,128)S(1)} %copy-done, f32[3,65536]{1,0:T(4,128)S(1)} %copy-done.5, ...), custom_call_target="tpu_custom_call" | custom-call | flops 8000000000 | bytes 1000000 | tf_op jit(solution)/shard_map/solve_points/pallas_call | solution.py:408
  66.0 0.0 copy-done.4
  66.0 9.2 %project_points.1 = (f32[4096,128]{1,0:T(8,128)}, f32[8,128]{1,0:T(8,128)S(1)}) custom-call(s32[1024]{0:T(1024)S(1)} %copy-done.11, s32[1024]{0:T(1024)S(1)} %copy-done.12, f32[1280,128]{1,0:T(8,128)S(1)} %bitcast.28, f32[1536,128]{1,0:T(8,128)S(1)} %bitcast.21, s32[2048,128]{1,0:T(8,128)S(1)} %bitcast.25, s32[2048,128]{1,0:T(8,128)S(1)} %bitcast.27, ...), custom_call_target="tpu_custom_call" | custom-call | flops 5000000000 | bytes 1000000 | tf_op jit(solution)/shard_map/project_points/pallas_call | solution.py:163
  75.2 14.4 %total_cost.1 = f32[1,1]{1,0:T(1,128)} custom-call(f32[8,128]{1,0:T(8,128)S(1)} %get-tuple-element.14.part_ref), custom_call_target="tpu_custom_call" | custom-call | flops 5000000000 | bytes 1000000 | tf_op jit(solution)/shard_map/total_cost/pallas_call | solution.py:288
  89.6 1.6 %bitcast_select_fusion = f32[3,65536]{1,0:T(4,128)} fusion(f32[3,65536]{1,0:T(4,128)S(1)} %copy-done, f32[1,3,512,128]{3,2,1,0:T(8,128)S(1)} %bitcast.22, pred[]{:T(512)S(6)} %eq.3), kind=kLoop, calls=%fused_computation | loop fusion | flops 196608 | bytes 2359297 | tf_op jit(solution)/shard_map/jit(_where)/select_n | solution.py:441
Async XLA Ops:
  1.3 0.7 copy-start.8
  2.0 20.3 %copy-start.1 = (bf16[18,262144]{1,0:T(8,128)(2,1)S(1)}, bf16[18,262144]{1,0:T(8,128)(2,1)}, u32[]{:S(2)}) copy-start(bf16[18,262144]{1,0:T(8,128)(2,1)} %cj_ref.1) | copy-start | bytes 28311556
  2.0 20.3 %copy-start.2 = (bf16[6,262144]{1,0:T(8,128)(2,1)S(1)}, bf16[6,262144]{1,0:T(8,128)(2,1)}, u32[]{:S(2)}) copy-start(bf16[6,262144]{1,0:T(8,128)(2,1)} %pj_ref.1) | copy-start | bytes 9437188
  2.0 20.3 %copy-start.6 = (s32[262144]{0:T(1024)S(1)}, s32[262144]{0:T(1024)}, u32[]{:S(2)}) copy-start(s32[262144]{0:T(1024)} %param.23) | copy-start | bytes 3145732
  2.0 20.4 %copy-start.7 = (s32[262144]{0:T(1024)S(1)}, s32[262144]{0:T(1024)}, u32[]{:S(2)}) copy-start(s32[262144]{0:T(1024)} %param.24) | copy-start | bytes 3145732
  2.0 20.4 %copy-start.9 = (f32[9,128]{1,0:T(8,128)S(1)}, f32[9,128]{1,0:T(8,128)}, u32[]{:S(2)}) copy-start(f32[9,128]{1,0:T(8,128)} %inc_ref.1) | copy-start | bytes 13828
  2.0 20.4 %copy-start.10 = (f32[9,128]{1,0:T(8,128)S(1)}, f32[9,128]{1,0:T(8,128)}, u32[]{:S(2)}) copy-start(f32[9,128]{1,0:T(8,128)} %cam_ref.3) | copy-start | bytes 13828
  2.0 20.4 %copy-start.11 = (s32[1024]{0:T(1024)S(1)}, s32[1024]{0:T(1024)}, u32[]{:S(2)}) copy-start(s32[1024]{0:T(1024)} %tb.3) | copy-start | bytes 12292
  2.0 20.4 %copy-start.12 = (s32[1024]{0:T(1024)S(1)}, s32[1024]{0:T(1024)}, u32[]{:S(2)}) copy-start(s32[1024]{0:T(1024)} %tp.3) | copy-start | bytes 12292
  22.4 23.8 %copy-start = (f32[3,65536]{1,0:T(4,128)S(1)}, f32[3,65536]{1,0:T(4,128)}, u32[]{:S(2)}) copy-start(f32[3,65536]{1,0:T(4,128)} %pts_hbm.1) | copy-start | bytes 2359300
  22.4 23.8 %copy-start.3 = (f32[9,65536]{1,0:T(8,128)S(1)}, f32[9,65536]{1,0:T(8,128)}, u32[]{:S(2)}) copy-start(f32[9,65536]{1,0:T(8,128)} %inv_hbm.1) | copy-start | bytes 7077892
  22.4 23.8 %copy-start.5 = (f32[3,65536]{1,0:T(4,128)S(1)}, f32[3,65536]{1,0:T(4,128)}, u32[]{:S(2)}) copy-start(f32[3,65536]{1,0:T(4,128)} %grad_hbm.1) | copy-start | bytes 2359300
  46.2 19.8 %copy-start.4 = (f32[2,262144]{1,0:T(2,128)S(1)}, f32[2,262144]{1,0:T(2,128)}, u32[]{:S(2)}) copy-start(f32[2,262144]{1,0:T(2,128)} %param.20) | copy-start | bytes 6291460

commit v6 on v5

--- a/solution.py
+++ b/solution.py
@@ -25,14 +25,13 @@
     return ref[pl.ds(first, 8, stride=0), :]
 
 PH=8; PL=32
-UN=16
+UN=32
 
 def reduce_body(chunk, blocks_n, tb, tp, word, inc_ref, cj_ref, pj_ref, oc_ref, op_ref, cam_ref, own_ref, out_ref, kept_ref, acc, jscr, pscr, wscr):
-    step = pl.program_id(0)
-    groups = chunk//GROUP
+    step = 0
+    groups = oc_ref.shape[0]//8
     row_id = lax.broadcasted_iota(jnp.int32,(8,128),0)
-    @pl.when(step==0)
-    def _():
+    if True:
         def zero(i,_):
             acc[pl.ds(pl.multiple_of(i*(PH*8),PH*8),PH*8),:] = jnp.zeros((PH*8,PL),F32)
             return 0
@@ -81,8 +80,7 @@
         for u in range(UN): scatter(i*UN+u, u)
         return 0
     lax.fori_loop(0, groups//UN, body, 0)
-    @pl.when(step==pl.num_programs(0)-1)
-    def _():
+    if True:
         def flush(i,_):
             for h in range(2):
                 n = 128//PL
@@ -99,35 +97,24 @@
     return pl.pallas_call(
         functools.partial(reduce_body, chunk, blocks_n),
         out_shape=(jax.ShapeDtypeStruct((3,npts//128,128),F32), jax.ShapeDtypeStruct((9,128),F32)),
-        grid_spec=pltpu.PrefetchScalarGridSpec(
-            num_scalar_prefetch=3, grid=(n//chunk,),
-            in_specs=[
-                pl.BlockSpec(inc.shape, lambda i,*_:(0,0)),
-                pl.BlockSpec((18,chunk), lambda i,*_:(0,i)),
-                pl.BlockSpec((6,chunk), lambda i,*_:(0,i)),
-                pl.BlockSpec((chunk//128,128), lambda i,*_:(i,0)),
-                pl.BlockSpec((chunk//128,128), lambda i,*_:(i,0)),
-                pl.BlockSpec((9,128), lambda i,*_:(0,0)),
-                pl.BlockSpec((9,128), lambda i,*_:(0,0)),
-            ],
-            out_specs=(pl.BlockSpec((3,npts//128,128), lambda i,*_:(0,0,0)), pl.BlockSpec((9,128), lambda i,*_:(0,0))),
+        in_specs=[pl.BlockSpec(memory_space=pltpu.SMEM)]*3+[pl.BlockSpec(memory_space=pltpu.VMEM)]*7,
+        out_specs=(pl.BlockSpec(memory_space=pltpu.VMEM), pl.BlockSpec(memory_space=pltpu.VMEM)),
             scratch_shapes=[pltpu.VMEM((blocks_n*PH*8,PL),F32), pltpu.VMEM((UN,192,128),F32), pltpu.VMEM((UN,64,128),F32), pltpu.VMEM((UN,64,128),F32)],
-        ),
         cost_estimate=pl.CostEstimate(flops=10000000000, bytes_accessed=1000000, transcendentals=0),
-        compiler_params=pltpu.CompilerParams(dimension_semantics=("arbitrary",), vmem_limit_bytes=28*1024*1024),
+        compiler_params=pltpu.CompilerParams(vmem_limit_bytes=28*1024*1024),
         name="reduce_points",
     )(tb,tp,word,inc,cj,pj,oc,op,cameras,increment)
 
 CT=10
-def project_body(chunk, tb, tp, cam_ref, pts_ref, oc_ref, op_ref, ob_ref, res_ref, cost_ref):
-    step=pl.program_id(0)
-    groups=chunk//GROUP
+TURN=16
+
+def project_body(tb, tp, word, cam_ref, pts_ref, oc_ref, op_ref, ob_ref, old_ref, res_hbm, acc_hbm, cost_ref, res_ref, acc_ref, sem):
+    turns=oc_ref.shape[0]//(8*TURN)
+    spans=old_ref.shape[1]//(128*turns)
     row_id=lax.broadcasted_iota(jnp.int32,(8,128),0)
-    @pl.when(step==0)
-    def _():
-        cost_ref[...]=jnp.zeros_like(cost_ref)
+    taken=jnp.broadcast_to(word[0]&1,(3,128))==1
     def one(g):
-        base=step*(chunk//TILE)+g*TPG
+        base=g*TPG
         cams=[tb[base+i]*CT for i in range(TPG)]
         pts=[tp[base+i]*2 for i in range(TPG)]
         at8=pl.ds(pl.multiple_of(g*8,8),8)
@@ -153,31 +140,42 @@
         ru=fac*u-ob_ref[o0,:]; rv=fac*v-ob_ref[o1,:]
         res_ref[o0,:]=ru; res_ref[o1,:]=rv
         return ru*ru+rv*rv
+    def out(i):
+        rows=pl.ds(pl.multiple_of(i*(TURN*16),TURN*16),TURN*16)
+        lanes=pl.ds(pl.multiple_of(i*(spans*128),spans*128),spans*128)
+        return (pltpu.make_async_copy(res_ref.at[rows],res_hbm.at[rows],sem.at[0,i]),
+                pltpu.make_async_copy(acc_ref.at[:,lanes],acc_hbm.at[:,lanes],sem.at[1,i]))
     def body(i,c):
-        for u in range(16): c=c+one(i*16+u)
+        for u in range(TURN): c=c+one(i*TURN+u)
+        for j in range(spans):
+            row=i*spans+j
+            lanes=pl.ds(pl.multiple_of(row*128,128),128)
+            new=jnp.concatenate([pts_ref[pl.ds(row+k*(spans*turns),1),:] for k in range(3)],axis=0)
+            acc_ref[:,lanes]=jnp.where(taken,new,old_ref[:,lanes])
+        for cp in out(i): cp.start()
         return c
-    cost_ref[...]+=lax.fori_loop(0,groups//16,body,jnp.zeros((8,128),F32))
-
-def project_points(cam, pts, oc, op, ob, tb, tp, chunk=65536):
+    cost_ref[...]=lax.fori_loop(0,turns,body,jnp.zeros((8,128),F32))
+    def finish(i,_):
+        for cp in out(i): cp.wait()
+        return 0
+    lax.fori_loop(0,turns,finish,0)
+
+def project_points(cam, pts, oc, op, ob, tb, tp, word, old):
     n=oc.shape[0]*128
+    turns=n//(GROUP*TURN)
+    smem=pl.BlockSpec(memory_space=pltpu.SMEM)
+    vmem=pl.BlockSpec(memory_space=pltpu.VMEM)
+    hbm=pl.BlockSpec(memory_space=pl.ANY)
     return pl.pallas_call(
-        functools.partial(project_body, chunk),
-        out_shape=(jax.ShapeDtypeStruct((n//64,128),F32), jax.ShapeDtypeStruct((8,128),F32)),
-        grid_spec=pltpu.PrefetchScalarGridSpec(
-            num_scalar_prefetch=2, grid=(n//chunk,),
-            in_specs=[
-                pl.BlockSpec(cam.shape, lambda i,*_:(0,0)),
-                pl.BlockSpec(pts.shape, lambda i,*_:(0,0)),
-                pl.BlockSpec((chunk//128,128), lambda i,*_:(i,0)),
-                pl.BlockSpec((chunk//128,128), lambda i,*_:(i,0)),
-                pl.BlockSpec((chunk//64,128), lambda i,*_:(i,0)),
-            ],
-            out_specs=(pl.BlockSpec((chunk//64,128), lambda i,*_:(i,0)), pl.BlockSpec((8,128), lambda i,*_:(0,0))),
-        ),
+        project_body,
+        out_shape=(jax.ShapeDtypeStruct((n//64,128),F32), jax.ShapeDtypeStruct(old.shape,F32), jax.ShapeDtypeStruct((8,128),F32)),
+        in_specs=[smem]*3+[vmem]*6,
+        out_specs=(hbm,hbm,vmem),
+        scratch_shapes=[pltpu.VMEM((n//64,128),F32), pltpu.VMEM(old.shape,F32), pltpu.SemaphoreType.DMA((2,turns))],
         cost_estimate=pl.CostEstimate(flops=5000000000, bytes_accessed=1000000, transcendentals=0),
-        compiler_params=pltpu.CompilerParams(dimension_semantics=("arbitrary",), vmem_limit_bytes=20*1024*1024),
+        compiler_params=pltpu.CompilerParams(vmem_limit_bytes=20*1024*1024),
         name="project_points",
-    )(tb,tp,cam,pts,oc,op,ob)
+    )(tb,tp,word,cam,pts,oc,op,ob,old)
 
 
 MESH = pl.DeviceIdType.MESH
@@ -434,11 +432,10 @@
     op2 = op.reshape(-1, 128)
     reduced, kept = reduce_points(gather_rows(increment), cj, pj, oc2, op2, tb, tp, accept.reshape(1), cameras, increment, points.shape[1])
     new, table = solve_points(reduced, cameras, increment, points, gradient, inverse)
-    res, cost = project_points(table, new.reshape(-1, 128), oc2, op2, rows_of(observed), tb, tp)
+    res, accepted, cost = project_points(table, new.reshape(-1, 128), oc2, op2, rows_of(observed), tb, tp, accept.reshape(1), points)
     n = observed.shape[1]
     residual = res.reshape(n // 128, 2, 128).transpose(1, 0, 2).reshape(2, n)
     total = total_cost(cost, 1.0 / (2.0 * n * lax.axis_size(PTS_CAM)))
-    accepted = jnp.where((accept & 1) == 1, new.reshape(3, -1), points)
     return residual, total, accepted, kept
 
 

time: 93.2 us -> 90.4 us (0.970)
  other arithmetic: 1.64 us -> 0 us
  Pallas kernels: 87.4 us -> 86.3 us
    select_n x1 -> x0, other arithmetic: 1.64 us -> none  [on_device(): accepted = jnp.where(accept & 1 == 1, new.reshape(3, -1), points)]
    pallas_call x1, Pallas kernels: 23.8 us -> 22.5 us  [reduce_points(): pl.pallas_call(functools.partial(reduce_body, chunk, blocks_n), out_shape...]
where the time goes in v6:
time: 90.4 us; the launch traced here: 90.2 us
  Pallas kernels  86.3 us (95%)
  between operations  3.21 us (4%)
    pallas_call x1, Pallas kernels, reduce_points(): pl.pallas_call(functools.partial(reduce_body, chunk, blocks_n), out_shape...  22.5 us
    pallas_call x1, Pallas kernels, gather_rows(): pl.pallas_call(gather_body, out_shape=jax.ShapeDtypeStruct((nx, ny, nc, n...  20.3 us
    pallas_call x1, Pallas kernels, solve_points(): pl.pallas_call(solve_body, out_shape=(jax.ShapeDtypeStruct(reduced.shape,...  19.7 us
    pallas_call x1, Pallas kernels, total_cost(): pl.pallas_call(functools.partial(cost_body, scale), out_shape=jax.ShapeDt...  14.5 us
    pallas_call x1, Pallas kernels, project_points(): pl.pallas_call(project_body, out_shape=(jax.ShapeDtypeStruct((n // 64, 12...  9.22 us

profile of v6, /device:TPU:1, one launch (start us, length us, event | category | flops | bytes accessed | tf_op | source)
XLA Modules:
  0.0 90.2 jit_solution(2934008659596300296)
XLA Ops:
  1.3 0.0 copy-start.8
  1.3 0.7 copy-done.8
  2.0 0.0 copy-start
  2.0 0.0 copy-start.1
  2.0 0.0 copy-start.5
  2.0 0.0 copy-start.6
  2.0 0.0 copy-start.9
  2.0 0.0 copy-start.10
  2.0 0.0 copy-start.11
  2.0 0.0 copy-start.12
  2.0 20.3 %gather_rows.1 = f32[4,4,2,4,9,1,128]{6,5,4,3,2,1,0:T(1,128)S(1)} custom-call(f32[9,128]{1,0:T(8,128)S(1)} %copy-done.8), custom_call_target="tpu_custom_call" | custom-call | flops 20000000000 | bytes 1000000 | tf_op jit(solution)/shard_map/gather_rows/pallas_call | solution.py:245
  22.3 0.0 copy-done
  22.3 0.0 copy-done.1
  22.3 0.0 copy-done.5
  22.3 0.0 copy-done.6
  22.3 0.0 copy-done.9
  22.4 0.0 copy-done.10
  22.4 0.0 copy-done.11
  22.4 0.0 copy-done.12
  22.4 0.0 copy-start.2
  22.4 0.0 copy-start.4
  22.4 0.0 copy-start.7
  22.4 22.5 %reduce_points.1 = (f32[3,512,128]{2,1,0:T(8,128)S(1)}, f32[9,128]{1,0:T(8,128)}) custom-call(s32[1024]{0:T(1024)S(1)} %copy-done.11, s32[1024]{0:T(1024)S(1)} %copy-done.12, s32[1]{0:T(128)} %bitcast.17.word, f32[1152,128]{1,0:T(8,128)S(1)} %bitcast.26, bf16[18,262144]{1,0:T(8,128)(2,1)S(1)} %copy-done, bf16[6,262144]{1,0:T(8,128)(2,1)S(1)} %copy-done.1, ...), custom_call_target="tpu_custom_call" | custom-call | flops 10000000000 | bytes 1000000 | tf_op jit(solution)/shard_map/reduce_points/pallas_call | solution.py:97
  44.9 0.0 copy-done.2
  44.9 0.0 copy-done.4
  44.9 0.0 copy-done.7
  44.9 0.0 copy-start.3
  45.0 19.7 %solve_points.1 = (f32[3,512,128]{2,1,0:T(8,128)S(1)}, f32[4,4,2,4,10,1,128]{6,5,4,3,2,1,0:T(1,128)S(1)}) custom-call(f32[3,512,128]{2,1,0:T(8,128)S(1)} %get-tuple-element.11.red_ref, f32[9,128]{1,0:T(8,128)S(1)} %copy-done.10, f32[9,128]{1,0:T(8,128)S(1)} %copy-done.9, f32[3,65536]{1,0:T(4,128)S(1)} %copy-done.7, f32[3,65536]{1,0:T(4,128)S(1)} %copy-done.4, ...), custom_call_target="tpu_custom_call" | custom-call | flops 8000000000 | bytes 1000000 | tf_op jit(solution)/shard_map/solve_points/pallas_call | solution.py:406
  64.7 0.0 copy-done.3
  64.7 9.2 %project_points.1 = (f32[4096,128]{1,0:T(8,128)}, f32[3,65536]{1,0:T(4,128)}, f32[8,128]{1,0:T(8,128)S(1)}) custom-call(s32[1024]{0:T(1024)S(1)} %copy-done.11, s32[1024]{0:T(1024)S(1)} %copy-done.12, s32[1]{0:T(128)} %bitcast.18.word, f32[1280,128]{1,0:T(8,128)S(1)} %bitcast.25, f32[1536,128]{1,0:T(8,128)S(1)} %bitcast.24, s32[2048,128]{1,0:T(8,128)S(1)} %bitcast.21, ...), custom_call_target="tpu_custom_call" | custom-call | flops 5000000000 | bytes 1000000 | tf_op jit(solution)/shard_map/project_points/pallas_call | solution.py:169
  73.9 14.5 %total_cost.1 = f32[1,1]{1,0:T(1,128)} custom-call(f32[8,128]{1,0:T(8,128)S(1)} %get-tuple-element.15.part_ref), custom_call_target="tpu_custom_call" | custom-call | flops 5000000000 | bytes 1000000 | tf_op jit(solution)/shard_map/total_cost/pallas_call | solution.py:286
Async XLA Ops:
  1.3 0.7 copy-start.8
  2.0 20.3 %copy-start = (bf16[18,262144]{1,0:T(8,128)(2,1)S(1)}, bf16[18,262144]{1,0:T(8,128)(2,1)}, u32[]{:S(2)}) copy-start(bf16[18,262144]{1,0:T(8,128)(2,1)} %cj_ref.1) | copy-start | bytes 28311556
  2.0 20.3 %copy-start.1 = (bf16[6,262144]{1,0:T(8,128)(2,1)S(1)}, bf16[6,262144]{1,0:T(8,128)(2,1)}, u32[]{:S(2)}) copy-start(bf16[6,262144]{1,0:T(8,128)(2,1)} %pj_ref.1) | copy-start | bytes 9437188
  2.0 20.3 %copy-start.5 = (s32[262144]{0:T(1024)S(1)}, s32[262144]{0:T(1024)}, u32[]{:S(2)}) copy-start(s32[262144]{0:T(1024)} %param.23) | copy-start | bytes 3145732
  2.0 20.4 %copy-start.6 = (s32[262144]{0:T(1024)S(1)}, s32[262144]{0:T(1024)}, u32[]{:S(2)}) copy-start(s32[262144]{0:T(1024)} %param.24) | copy-start | bytes 3145732
  2.0 20.4 %copy-start.9 = (f32[9,128]{1,0:T(8,128)S(1)}, f32[9,128]{1,0:T(8,128)}, u32[]{:S(2)}) copy-start(f32[9,128]{1,0:T(8,128)} %inc_ref.1) | copy-start | bytes 13828
  2.0 20.4 %copy-start.10 = (f32[9,128]{1,0:T(8,128)S(1)}, f32[9,128]{1,0:T(8,128)}, u32[]{:S(2)}) copy-start(f32[9,128]{1,0:T(8,128)} %cam_ref.3) | copy-start | bytes 13828
  2.0 20.4 %copy-start.11 = (s32[1024]{0:T(1024)S(1)}, s32[1024]{0:T(1024)}, u32[]{:S(2)}) copy-start(s32[1024]{0:T(1024)} %tb.3) | copy-start | bytes 12292
  2.0 20.4 %copy-start.12 = (s32[1024]{0:T(1024)S(1)}, s32[1024]{0:T(1024)}, u32[]{:S(2)}) copy-start(s32[1024]{0:T(1024)} %tp.3) | copy-start | bytes 12292
  22.4 22.6 %copy-start.2 = (f32[9,65536]{1,0:T(8,128)S(1)}, f32[9,65536]{1,0:T(8,128)}, u32[]{:S(2)}) copy-start(f32[9,65536]{1,0:T(8,128)} %inv_hbm.1) | copy-start | bytes 7077892
  22.4 22.5 %copy-start.4 = (f32[3,65536]{1,0:T(4,128)S(1)}, f32[3,65536]{1,0:T(4,128)}, u32[]{:S(2)}) copy-start(f32[3,65536]{1,0:T(4,128)} %grad_hbm.1) | copy-start | bytes 2359300
  22.4 22.5 %copy-start.7 = (f32[3,65536]{1,0:T(4,128)S(1)}, f32[3,65536]{1,0:T(4,128)}, u32[]{:S(2)}) copy-start(f32[3,65536]{1,0:T(4,128)} %old_ref.1) | copy-start | bytes 2359300
  44.9 19.8 %copy-start.3 = (f32[2,262144]{1,0:T(2,128)S(1)}, f32[2,262144]{1,0:T(2,128)}, u32[]{:S(2)}) copy-start(f32[2,262144]{1,0:T(2,128)} %param.20) | copy-start | bytes 6291460

commit v7 on v6

--- a/solution.py
+++ b/solution.py
@@ -265,21 +265,25 @@
     x, y, c, z = [lax.axis_index(a) for a in (X, Y, CORE, CAM)]
     peers = cost_peers()
     greet(peers[0] + peers[1])
-    value = part_ref[...]
+    value = jnp.sum(part_ref[...], axis=0, keepdims=True)
     slot = 0
+    sent = []
     for stage, (me, count) in enumerate(((y * 4 + z, 16), (x * 2 + c, 8))):
-        buf[stage, pl.ds(pl.multiple_of(me * 8, 8), 8), :] = value
-        own = buf.at[stage, pl.ds(pl.multiple_of(me * 8, 8), 8)]
+        buf[stage, me] = value
+        own = buf.at[stage, me]
         copies = []
         for p in peers[stage]:
             copies.append(send(own, own, send_sem.at[slot], recv_sem.at[slot], p))
             slot += 1
         for cp in copies:
-            cp.wait()
-        value = buf[stage, 0:8, :]
+            cp.wait_recv()
+        sent += copies
+        value = buf[stage, 0]
         for k in range(1, count):
-            value = value + buf[stage, k * 8:k * 8 + 8, :]
+            value = value + buf[stage, k]
     out_ref[...] = jnp.sum(value, axis=(0, 1), keepdims=True) * scale
+    for cp in sent:
+        cp.wait_send()
 
 
 def total_cost(part, scale):
@@ -288,7 +292,7 @@
         out_shape=jax.ShapeDtypeStruct((1, 1), F32),
         in_specs=[pl.BlockSpec(memory_space=pltpu.VMEM)],
         out_specs=pl.BlockSpec(memory_space=pltpu.VMEM),
-        scratch_shapes=[pltpu.VMEM((2, 128, 128), F32), pltpu.SemaphoreType.DMA((22,)), pltpu.SemaphoreType.DMA((22,))],
+        scratch_shapes=[pltpu.VMEM((2, 16, 1, 128), F32), pltpu.SemaphoreType.DMA((22,)), pltpu.SemaphoreType.DMA((22,))],
         cost_estimate=pl.CostEstimate(flops=5000000000, bytes_accessed=1000000, transcendentals=0),
         compiler_params=pltpu.CompilerParams(collective_id=1, has_side_effects=True, vmem_limit_bytes=4*1024*1024),
         name="total_cost",

time: 90.4 us -> 89.8 us (level)
  no operation moved by 1% of the time
where the time goes in v7:
time: 89.8 us; the launch traced here: 89.6 us
  Pallas kernels  85.6 us (95%)
  between operations  3.21 us (4%)
    pallas_call x1, Pallas kernels, reduce_points(): pl.pallas_call(functools.partial(reduce_body, chunk, blocks_n), out_shape...  22.5 us
    pallas_call x1, Pallas kernels, gather_rows(): pl.pallas_call(gather_body, out_shape=jax.ShapeDtypeStruct((nx, ny, nc, n...  20.3 us
    pallas_call x1, Pallas kernels, solve_points(): pl.pallas_call(solve_body, out_shape=(jax.ShapeDtypeStruct(reduced.shape,...  19.7 us
    pallas_call x1, Pallas kernels, total_cost(): pl.pallas_call(functools.partial(cost_body, scale), out_shape=jax.ShapeDt...  13.9 us
    pallas_call x1, Pallas kernels, project_points(): pl.pallas_call(project_body, out_shape=(jax.ShapeDtypeStruct((n // 64, 12...  9.2 us

profile of v7, /device:TPU:1, one launch (start us, length us, event | category | flops | bytes accessed | tf_op | source)
XLA Modules:
  0.0 89.6 jit_solution(4845871946405342412)
XLA Ops:
  1.3 0.0 copy-start.8
  1.3 0.7 copy-done.8
  2.0 0.0 copy-start
  2.0 0.0 copy-start.1
  2.0 0.0 copy-start.5
  2.0 0.0 copy-start.6
  2.0 0.0 copy-start.9
  2.0 0.0 copy-start.10
  2.0 0.0 copy-start.11
  2.0 0.0 copy-start.12
  2.0 20.3 %gather_rows.1 = f32[4,4,2,4,9,1,128]{6,5,4,3,2,1,0:T(1,128)S(1)} custom-call(f32[9,128]{1,0:T(8,128)S(1)} %copy-done.8), custom_call_target="tpu_custom_call" | custom-call | flops 20000000000 | bytes 1000000 | tf_op jit(solution)/shard_map/gather_rows/pallas_call | solution.py:245
  22.3 0.0 copy-done
  22.3 0.0 copy-done.1
  22.3 0.0 copy-done.5
  22.3 0.0 copy-done.6
  22.3 0.0 copy-done.9
  22.4 0.0 copy-done.10
  22.4 0.0 copy-done.11
  22.4 0.0 copy-done.12
  22.4 0.0 copy-start.2
  22.4 0.0 copy-start.4
  22.4 0.0 copy-start.7
  22.4 22.5 %reduce_points.1 = (f32[3,512,128]{2,1,0:T(8,128)S(1)}, f32[9,128]{1,0:T(8,128)}) custom-call(s32[1024]{0:T(1024)S(1)} %copy-done.11, s32[1024]{0:T(1024)S(1)} %copy-done.12, s32[1]{0:T(128)} %bitcast.17.word, f32[1152,128]{1,0:T(8,128)S(1)} %bitcast.26, bf16[18,262144]{1,0:T(8,128)(2,1)S(1)} %copy-done, bf16[6,262144]{1,0:T(8,128)(2,1)S(1)} %copy-done.1, ...), custom_call_target="tpu_custom_call" | custom-call | flops 10000000000 | bytes 1000000 | tf_op jit(solution)/shard_map/reduce_points/pallas_call | solution.py:97
  44.9 0.0 copy-done.2
  44.9 0.0 copy-done.4
  44.9 0.0 copy-done.7
  44.9 0.0 copy-start.3
  44.9 19.7 %solve_points.1 = (f32[3,512,128]{2,1,0:T(8,128)S(1)}, f32[4,4,2,4,10,1,128]{6,5,4,3,2,1,0:T(1,128)S(1)}) custom-call(f32[3,512,128]{2,1,0:T(8,128)S(1)} %get-tuple-element.11.red_ref, f32[9,128]{1,0:T(8,128)S(1)} %copy-done.10, f32[9,128]{1,0:T(8,128)S(1)} %copy-done.9, f32[3,65536]{1,0:T(4,128)S(1)} %copy-done.7, f32[3,65536]{1,0:T(4,128)S(1)} %copy-done.4, ...), custom_call_target="tpu_custom_call" | custom-call | flops 8000000000 | bytes 1000000 | tf_op jit(solution)/shard_map/solve_points/pallas_call | solution.py:410
  64.7 0.0 copy-done.3
  64.7 9.2 %project_points.1 = (f32[4096,128]{1,0:T(8,128)}, f32[3,65536]{1,0:T(4,128)}, f32[8,128]{1,0:T(8,128)S(1)}) custom-call(s32[1024]{0:T(1024)S(1)} %copy-done.11, s32[1024]{0:T(1024)S(1)} %copy-done.12, s32[1]{0:T(128)} %bitcast.18.word, f32[1280,128]{1,0:T(8,128)S(1)} %bitcast.25, f32[1536,128]{1,0:T(8,128)S(1)} %bitcast.24, s32[2048,128]{1,0:T(8,128)S(1)} %bitcast.21, ...), custom_call_target="tpu_custom_call" | custom-call | flops 5000000000 | bytes 1000000 | tf_op jit(solution)/shard_map/project_points/pallas_call | solution.py:169
  73.9 13.9 %total_cost.1 = f32[1,1]{1,0:T(1,128)} custom-call(f32[8,128]{1,0:T(8,128)S(1)} %get-tuple-element.15.part_ref), custom_call_target="tpu_custom_call" | custom-call | flops 5000000000 | bytes 1000000 | tf_op jit(solution)/shard_map/total_cost/pallas_call | solution.py:290
Async XLA Ops:
  1.3 0.7 copy-start.8
  2.0 20.3 %copy-start = (bf16[18,262144]{1,0:T(8,128)(2,1)S(1)}, bf16[18,262144]{1,0:T(8,128)(2,1)}, u32[]{:S(2)}) copy-start(bf16[18,262144]{1,0:T(8,128)(2,1)} %cj_ref.1) | copy-start | bytes 28311556
  2.0 20.3 %copy-start.1 = (bf16[6,262144]{1,0:T(8,128)(2,1)S(1)}, bf16[6,262144]{1,0:T(8,128)(2,1)}, u32[]{:S(2)}) copy-start(bf16[6,262144]{1,0:T(8,128)(2,1)} %pj_ref.1) | copy-start | bytes 9437188
  2.0 20.3 %copy-start.5 = (s32[262144]{0:T(1024)S(1)}, s32[262144]{0:T(1024)}, u32[]{:S(2)}) copy-start(s32[262144]{0:T(1024)} %param.23) | copy-start | bytes 3145732
  2.0 20.4 %copy-start.6 = (s32[262144]{0:T(1024)S(1)}, s32[262144]{0:T(1024)}, u32[]{:S(2)}) copy-start(s32[262144]{0:T(1024)} %param.24) | copy-start | bytes 3145732
  2.0 20.4 %copy-start.9 = (f32[9,128]{1,0:T(8,128)S(1)}, f32[9,128]{1,0:T(8,128)}, u32[]{:S(2)}) copy-start(f32[9,128]{1,0:T(8,128)} %inc_ref.1) | copy-start | bytes 13828
  2.0 20.4 %copy-start.10 = (f32[9,128]{1,0:T(8,128)S(1)}, f32[9,128]{1,0:T(8,128)}, u32[]{:S(2)}) copy-start(f32[9,128]{1,0:T(8,128)} %cam_ref.3) | copy-start | bytes 13828
  2.0 20.4 %copy-start.11 = (s32[1024]{0:T(1024)S(1)}, s32[1024]{0:T(1024)}, u32[]{:S(2)}) copy-start(s32[1024]{0:T(1024)} %tb.3) | copy-start | bytes 12292
  2.0 20.4 %copy-start.12 = (s32[1024]{0:T(1024)S(1)}, s32[1024]{0:T(1024)}, u32[]{:S(2)}) copy-start(s32[1024]{0:T(1024)} %tp.3) | copy-start | bytes 12292
  22.4 22.5 %copy-start.2 = (f32[9,65536]{1,0:T(8,128)S(1)}, f32[9,65536]{1,0:T(8,128)}, u32[]{:S(2)}) copy-start(f32[9,65536]{1,0:T(8,128)} %inv_hbm.1) | copy-start | bytes 7077892
  22.4 22.5 %copy-start.4 = (f32[3,65536]{1,0:T(4,128)S(1)}, f32[3,65536]{1,0:T(4,128)}, u32[]{:S(2)}) copy-start(f32[3,65536]{1,0:T(4,128)} %grad_hbm.1) | copy-start | bytes 2359300
  22.4 22.5 %copy-start.7 = (f32[3,65536]{1,0:T(4,128)S(1)}, f32[3,65536]{1,0:T(4,128)}, u32[]{:S(2)}) copy-start(f32[3,65536]{1,0:T(4,128)} %old_ref.1) | copy-start | bytes 2359300
  44.9 19.8 %copy-start.3 = (f32[2,262144]{1,0:T(2,128)S(1)}, f32[2,262144]{1,0:T(2,128)}, u32[]{:S(2)}) copy-start(f32[2,262144]{1,0:T(2,128)} %param.20) | copy-start | bytes 6291460
